TPU v7x, 32 devices: a whole 2x2x4 slice. The times are simulated.
32 devices in a mesh: gx: 2 (over y), gy: 4 (over z), gz: 4 (over x, core).
Axes of the slice: x: 2, y: 2, z: 4, core: 2. Of those that a mesh axis runs over, the one named last changes fastest.
Arguments:
- density: float32 [24, 64, 512], P('gx', 'gy', 'gz'), may hold values from 0.5 to 8
- potential: float32 [24, 64, 512], P('gx', 'gy', 'gz'), may hold values from -6 to 6
Outputs:
- corrected: float32 [24, 64, 512], P('gx', 'gy', 'gz')
All inputs are finite; a program needn't handle non-finite values.
Results may differ from a plain program's by a relative error of at most 0.00005.
Values sent between devices are 32-bit elements; how exact they have to be, the bound alone decides.
A program may use at most 64 MiB of HBM per device.

v0:
```python
import functools
import numpy as np
import jax
import jax.numpy as jnp
from jax import lax
from jax.experimental import pallas as pl
from jax.experimental.pallas import tpu as pltpu
from jax.sharding import PartitionSpec as P

SWEEPS = 2
HI = lax.Precision.HIGHEST
MESH = pl.DeviceIdType.MESH
R = 8


def table(count):
    modes = (np.arange(count) + 1) // 2
    angle = 2 * np.pi * np.outer(np.arange(count), modes) / count
    q = np.where(np.arange(count) % 2 == 1, np.cos(angle), np.sin(angle)) * np.sqrt(2 / count)
    q = np.where(2 * modes == count, np.cos(angle) / np.sqrt(count), q)
    q[:, 0] = 1 / np.sqrt(count)
    return q, 2 - 2 * np.cos(2 * np.pi * modes / count)


def coarse_operator(nx, ny, nz, wx, wy, wz):
    qx, lx = table(nx)
    qy, ly = table(ny)
    qz, lz = table(nz)
    q = np.kron(np.kron(qx, qy), qz)
    lam = wx * lx[:, None, None] + wy * ly[None, :, None] + wz * lz[None, None, :]
    lam = lam.reshape(-1)
    inv = np.concatenate([[0.0], -1.0 / lam[1:]])
    return ((q * inv) @ q.T).astype(np.float32)


def kernel(
    dims, den_hbm, pot_hbm, op_hbm, out_ref, op_ref,
    own, pm, pa, pb, den, lv, ea, eb, e2, f2, gat, cv,
    pk_p, pk_l, pk_e, pk_f, rk_p, rk_l, rk_e, rk_f,
    ssem, rsem, gs, gr, lsem,
):
    nx, ny, nz, X, Y, Z = dims
    n = nx * ny * nz
    x1, y1, z1 = X // 2, Y // 2, Z // 2
    ix, iy, iz = lax.axis_index("gx"), lax.axis_index("gy"), lax.axis_index("gz")
    me = (ix * ny + iy) * nz + iz

    def around(i, count):
        return [i] + [jnp.where(i + o >= count, i + o - count, i + o) for o in range(1, count)]

    xs, ys, zs = around(ix, nx), around(iy, ny), around(iz, nz)

    def device(o):
        if isinstance(o, int):
            return (xs[o // (ny * nz)], ys[o // nz % ny], zs[o % nz])
        ox, oy, oz = o // (ny * nz), (o // nz) % ny, o % nz
        return (lax.rem(ix + ox, nx), lax.rem(iy + oy, ny), lax.rem(iz + oz, nz))

    def each_other(step):
        if n <= 64:
            for o in range(1, n):
                step(o, 0)
        else:
            lax.fori_loop(1, n, step, 0)

    load_p = pltpu.make_async_copy(pot_hbm, own, lsem.at[0])
    load_d = pltpu.make_async_copy(den_hbm, den.at[pl.ds(6, X), pl.ds(R, Y), pl.ds(0, Z)], lsem.at[1])
    load_p.start()
    load_d.start()
    load_op = pltpu.make_async_copy(op_hbm, op_ref, lsem.at[2])
    load_op.start()

    barrier = pltpu.get_barrier_semaphore()

    def greet(o, carry):
        pl.semaphore_signal(barrier, inc=1, device_id=device(o), device_id_type=MESH)
        return carry

    near = max(nx, ny, nz) <= 5
    steps = sorted({
        (dx % nx * ny + dy % ny) * nz + dz % nz
        for dx in (-1, 0, 1) for dy in (-1, 0, 1) for dz in (-1, 0, 1)
    } - {0})
    if near:
        for o in steps:
            greet(o, 0)
    else:
        each_other(greet)
    load_p.wait()
    load_d.wait()
    odd = (
        lax.broadcasted_iota(jnp.int32, (Y, Z), 0) + lax.broadcasted_iota(jnp.int32, (Y, Z), 1)
    ) % 2 == 1
    for j in range(X // 2):
        pm[3 + j, R : R + Y, 0:Z] = jnp.where(odd, own[2 * j], own[2 * j + 1])

    sems = iter(range(200))

    def pack(items, pk):
        base = 0
        sy = items[0][3][1]
        lane = lax.broadcasted_iota(jnp.int32, (sy, 128), 1)
        head = tail = jnp.zeros((sy, 128), jnp.float32)
        for buf, h, H, (sx, sy, sz), deep in items:
            for q in range(sx):
                v = buf[H + q, R : R + sy, 0:128]
                at = base + q * deep
                inside = (lane >= at) & (lane < at + deep)
                tail = jnp.where(inside, pltpu.roll(v, (at - (sz - deep)) % 128, 1), tail)
                head = jnp.where(inside, pltpu.roll(v, at, 1) if at else v, head)
            base += sx * deep
        assert base <= 128
        pk[0] = tail
        pk[1] = head

    def once(h, H, sx):
        return nx == 2 and 2 * h > sx and H >= sx

    def exchange(items, pk, rk):
        copies = []

        def send(src, dst, dx, dy, dz):
            k = next(sems)
            to = (xs[dx], ys[dy], zs[dz])
            copy = pltpu.make_async_remote_copy(
                src_ref=src, dst_ref=dst, send_sem=ssem.at[k], recv_sem=rsem.at[k],
                device_id=to, device_id_type=MESH,
            )
            copy.start()
            copies.append(copy)

        sy = items[0][3][1]
        rows_from = {0: pl.ds(R, sy), 1: pl.ds(sy, R), -1: pl.ds(R, R)}
        rows_to = {0: pl.ds(R, sy), 1: pl.ds(0, R), -1: pl.ds(R + sy, R)}
        for dx in (1, -1, 0):
            for dy in (1, -1, 0):
                for dz in (1, -1):
                    if dx == -1 and nx == 2:
                        continue
                    side = 0 if dz == 1 else 1
                    count = R if dy else sy
                    first = sy - R if dy == 1 else 0
                    send(
                        pk.at[side, pl.ds(first, count)],
                        rk.at[side, 1 - dx, 1 - dy, pl.ds(0, count)],
                        dx, dy, dz,
                    )
                if dx == 0 and dy == 0:
                    continue
                for buf, h, H, (sx, sy, sz), deep in items:
                    if once(h, H, sx):
                        if dx == -1:
                            continue
                        h = sx if dx else h
                    p_from = {0: pl.ds(H, sx), 1: pl.ds(H + sx - h, h), -1: pl.ds(H, h)}[dx]
                    p_to = {0: pl.ds(H, sx), 1: pl.ds(H - h, h), -1: pl.ds(H + sx, h)}[dx]
                    lanes = pl.ds(0, 128)
                    send(buf.at[p_from, rows_from[dy], lanes], buf.at[p_to, rows_to[dy], lanes], dx, dy, 0)
        return functools.partial(finish, items, rk, copies)

    def finish(items, rk, copies):
        for copy in copies:
            copy.wait()
        received = {}
        for group in range(3):
            slot = 0 if nx == 2 and group == 2 else group
            for side in range(2):
                received[side, group] = jnp.concatenate(
                    [rk[side, slot, 0, 0:R], rk[side, slot, 1], rk[side, slot, 2, 0:R]], axis=0
                )
        base = 0
        for buf, h, H, (sx, sy, sz), deep in items:
            rows = sy + 2 * R
            lane = lax.broadcasted_iota(jnp.int32, (rows, 128), 1)
            wide = sz == 128
            assert not (wide and once(h, H, sx))
            put = 0 if wide else sz
            for j in range(sx + 2 * h):
                group, q = (0, sx - h + j) if j < h else ((1, j - h) if j < h + sx else (2, j - h - sx))
                at = base + q * deep
                edge = jnp.where(
                    lane >= 112,
                    pltpu.roll(received[0, group], (128 - deep - at) % 128, 1),
                    pltpu.roll(received[1, group], (put - at) % 128, 1),
                )
                if wide:
                    buf[H - h + j, :, 128:256] = edge
                else:
                    at = H - sx + q if group == 2 and once(h, H, sx) else H - h + j
                    buf[H - h + j] = jnp.where(lane < sz, buf[at], edge)
            base += sx * deep

    sixth = jnp.float32(1.0 / 6.0)

    def masks(rows, lanes):
        even = (
            lax.broadcasted_iota(jnp.int32, (rows, lanes), 0)
            + lax.broadcasted_iota(jnp.int32, (rows, lanes), 1)
        ) % 2 == 0
        return even, jnp.logical_not(even)

    def beside(a, p, c, index=lambda p: p):
        rows, lanes = c.shape
        t = a[index(p - 1)] + a[index(p + 1)]
        t = t + (pltpu.roll(c, 1, 0) + pltpu.roll(c, rows - 1, 0))
        return t + (pltpu.roll(c, 1, 1) + pltpu.roll(c, lanes - 1, 1))

    def half(a, b, s, lo, hi, H, off, colour, mask, shift=None, index=lambda p: p):
        for p in range(lo, hi):
            c = a[index(p)]
            t = beside(a, p, c, index) - s[p + off]
            if shift is not None:
                t = t + shift
            b[p] = jnp.where(mask[(p - H + colour) % 2], t * sixth, c)

    fine_mask = masks(Y + 2 * R, 2 * Z)
    one_mask = masks(y1 + 2 * R, 128)

    first = [(pm, 3, 3, (X // 2, Y, Z), 5), (den, 4, 6, (X, Y, Z), 4)]
    pack(first, pk_p)
    pl.semaphore_wait(barrier, len(steps) if near else n - 1)
    exchange(first, pk_p, rk_p)()
    for k, (a, b) in enumerate(((pm, pb), (pb, pa), (pa, pb), (pb, pa))):
        d = 4 - k
        index = (lambda p: p // 2) if k == 0 else (lambda p: p)
        half(a, b, den, 6 - d, 6 + X + d, 6, 0, k % 2, fine_mask, None, index)
    pairs = []
    total = jnp.zeros((Y, Z), jnp.float32)
    for q in range(x1):
        both = None
        for p in (6 + 2 * q, 7 + 2 * q):
            c = pa[p]
            left = (den[p] - (beside(pa, p, c) - 6.0 * c))[R : R + Y, 0:Z]
            both = left if both is None else both + left
            total = total + den[p, R : R + Y, 0:Z]
        f2[2 + q, R : R + Y, 0:Z] = jnp.where(
            odd, pa[6 + 2 * q, R : R + Y, 0:Z], pa[7 + 2 * q, R : R + Y, 0:Z]
        )
        pairs.append(both)
    def halves(shape, dim, start=0):
        i = [lax.broadcasted_iota(jnp.int32, shape, k) for k in (0, 1)]
        return jnp.where((i[dim] >> 1) + start == i[1 - dim], 1.0, 0.0).astype(jnp.float32)

    to_z, to_y = halves((Z, 128), 0), halves((x1 * y1, x1 * Y), 1)
    from_z, from_y = halves((128, 2 * Z), 1), halves((Y + 2 * R, y1 + 2 * R), 0, R // 2)
    stacked = jnp.concatenate(pairs, axis=0)
    stacked = jnp.dot(stacked, to_z, precision=HI, preferred_element_type=jnp.float32)
    one = jnp.dot(to_y, stacked, precision=HI, preferred_element_type=jnp.float32) * 0.5
    for q in range(x1):
        lv[6 + q, R : R + y1, :] = one[q * y1 : (q + 1) * y1]

    second = [(lv, 5, 6, (x1, y1, z1), 5)]
    pack(second, pk_l)
    finish_second = exchange(second, pk_l, rk_l)
    fourth = [(f2, 2, 2, (X // 2, Y, Z), 4)]
    pack(fourth, pk_f)
    finish_fourth = exchange(fourth, pk_f, rk_f)
    def whole_sum(v):
        return jnp.sum(jnp.sum(v, axis=0, keepdims=True), axis=1, keepdims=True)

    gat[me, :, 128:256] = jnp.broadcast_to(whole_sum(total), (1, 128))
    finish_second()
    for p in range(6 - 4, 6 + x1 + 4):
        ea[p] = jnp.where(one_mask[p % 2], lv[p] * -sixth, 0.0)
    for k, (a, b) in enumerate(((ea, eb), (eb, ea), (ea, eb))):
        d = 3 - k
        half(a, b, lv, 6 - d, 6 + x1 + d, 6, 0, (k + 1) % 2, one_mask)
    acc = jnp.zeros((y1, 128), jnp.float32)
    for p in range(6, 6 + x1):
        c = eb[p]
        acc = acc + (lv[p] - (beside(eb, p, c) - 6.0 * c))[R : R + y1]
    for j in range(x1 // 2):
        e2[3 + j, R : R + y1, :] = jnp.where(
            odd[0:y1], eb[6 + 2 * j, R : R + y1], eb[7 + 2 * j, R : R + y1]
        )
    lane = lax.broadcasted_iota(jnp.int32, (y1, 128), 1)
    acc = jnp.where(lane < z1, acc, 0.0)

    gat[me, :, 0:128] = jnp.broadcast_to(whole_sum(acc), (1, 128))

    def spread(o, carry):
        pltpu.make_async_remote_copy(
            src_ref=gat.at[me], dst_ref=gat.at[me], send_sem=gs, recv_sem=gr,
            device_id=device(o), device_id_type=MESH,
        ).start()
        return carry

    each_other(spread)
    third = [(e2, 3, 3, (x1 // 2, y1, z1), 6)]
    pack(third, pk_e)
    finish_third = exchange(third, pk_e, rk_e)
    finish_fourth()
    finish_third()
    others = gat.at[pl.ds(0, n - 1)]
    pltpu.make_async_copy(others, others, gs).wait()
    pltpu.make_async_copy(others, others, gr).wait()

    load_op.wait()
    values = gat[:, 0, :]
    blocks = values[:, 0:128]
    mean = jnp.sum(values[:, 128:256], axis=0, keepdims=True) / jnp.float32(n * X * Y * Z)
    blocks = blocks - jnp.sum(blocks, axis=0, keepdims=True) / jnp.float32(n)
    cv[...] = jnp.dot(op_ref[...], blocks, precision=HI, preferred_element_type=jnp.float32)
    row = lax.broadcasted_iota(jnp.int32, (y1 + 2 * R, 128), 0)
    lane = lax.broadcasted_iota(jnp.int32, (y1 + 2 * R, 128), 1)
    maps = []
    for dx in (-1, 0, 1):
        by_row = []
        for dy in (-1, 0, 1):
            vals = []
            for dz in (-1, 0, 1):
                at = (xs[dx] * ny + ys[dy]) * nz
                vals.append(cv[pl.ds(at + zs[dz], 1), :])
            by_row.append(jnp.where(lane < z1, vals[1], jnp.where(lane < (z1 + 128) // 2, vals[2], vals[0])))
        maps.append(jnp.where(row < R, by_row[0], jnp.where(row < R + y1, by_row[1], by_row[2])))
    for p in range(0, x1 + 12):
        which = 0 if p < 6 else (1 if p < 6 + x1 else 2)
        ea[p] = e2[p // 2] + (maps[which] + mean * jnp.float32(8.0 / 3.0))
    for k, (a, b) in enumerate(((ea, eb), (eb, ea), (ea, eb), (eb, ea))):
        d = 5 - k
        half(a, b, lv, 6 - d, 6 + x1 + d, 6, 0, k % 2, one_mask, 4.0 * mean)

    mean2 = jnp.concatenate([mean, mean], axis=1)
    for q in range(4, 6 + x1 + 2):
        wide = jnp.dot(ea[q], from_z, precision=HI, preferred_element_type=jnp.float32)
        wide = jnp.dot(from_y, wide, precision=HI, preferred_element_type=jnp.float32)
        wide = wide + mean2 * jnp.float32(2.0 / 3.0)
        for p in (2 * (q - 4), 2 * (q - 4) + 1):
            pb[p] = f2[p // 2] + wide
    for k, (a, b) in enumerate(((pb, pa), (pa, pb), (pb, pa))):
        d = 3 - k
        half(a, b, den, 4 - d, 4 + X + d, 4, 2, k % 2, fine_mask, mean2)
    for p in range(4, 4 + X):
        c = pa[p]
        t = (beside(pa, p, c) - den[p + 2] + mean2) * sixth
        out_ref[p - 4] = jnp.where(fine_mask[(p - 3) % 2], t, c)[R : R + Y, 0:Z]


def body(dims, density, potential):
    nx, ny, nz, X, Y, Z = dims
    n = nx * ny * nz
    x1, y1, z1 = X // 2, Y // 2, Z // 2
    op = coarse_operator(nx, ny, nz, float(y1 * z1), float(x1 * z1), float(x1 * y1))
    rows, rows1 = Y + 2 * R, y1 + 2 * R
    f32 = jnp.float32
    fine, one = (Y, 128), (y1, 128)
    vmem = pl.BlockSpec(memory_space=pltpu.VMEM)
    return pl.pallas_call(
        functools.partial(kernel, dims),
        out_shape=jax.ShapeDtypeStruct((X, Y, Z), f32),
        in_specs=[pl.BlockSpec(memory_space=pl.ANY)] * 3,
        out_specs=vmem,
        scratch_shapes=[
            pltpu.VMEM((n, n), f32),
            pltpu.VMEM((X, Y, Z), f32),
            pltpu.VMEM((X // 2 + 6, rows, 2 * Z), f32),
            pltpu.VMEM((X + 12, rows, 2 * Z), f32),
            pltpu.VMEM((X + 12, rows, 2 * Z), f32),
            pltpu.VMEM((X + 12, rows, 2 * Z), f32),
            pltpu.VMEM((x1 + 12, rows1, 128), f32),
            pltpu.VMEM((x1 + 12, rows1, 128), f32),
            pltpu.VMEM((x1 + 12, rows1, 128), f32),
            pltpu.VMEM((x1 // 2 + 6, rows1, 128), f32),
            pltpu.VMEM((X // 2 + 4, rows, 2 * Z), f32),
            pltpu.VMEM((n, 1, 256), f32),
            pltpu.VMEM((n, 128), f32),
        ]
        + [pltpu.VMEM(lead + s, f32) for lead in ((2,), (2, 3, 3)) for s in (fine, one, one, fine)]
        + [
            pltpu.SemaphoreType.DMA((120,)),
            pltpu.SemaphoreType.DMA((120,)),
            pltpu.SemaphoreType.DMA,
            pltpu.SemaphoreType.DMA,
            pltpu.SemaphoreType.DMA((3,)),
        ],
        compiler_params=pltpu.CompilerParams(collective_id=0, has_side_effects=True),
        name="vcycle",
    )(density, potential, op)


def solution(mesh):
    nx, ny, nz = (mesh.shape[a] for a in ("gx", "gy", "gz"))

    def run(density, potential):
        return body((nx, ny, nz) + density.shape, density, potential)

    spec = P("gx", "gy", "gz")
    return jax.shard_map(run, mesh=mesh, in_specs=(spec, spec), out_specs=spec, check_vma=False)
```

profile of v0, /device:TPU:0, one launch (start us, length us, event | category | flops | bytes accessed | tf_op | source)
XLA Modules:
  0.0 36.4 jit_solution(16150756542611232096)
XLA Ops:
  0.0 34.9 %vcycle.1 = f32[12,16,128]{2,1,0:T(8,128)} custom-call(f32[12,16,128]{2,1,0:T(8,128)} %den_hbm.1, f32[12,16,128]{2,1,0:T(8,128)} %pot_hbm.1, f32[32,32]{1,0:T(8,128)} %constant.2.clone.op_hbm), custom_call_target="tpu_custom_call" | custom-call | tf_op jit(solution)/shard_map/vcycle/pallas_call | solution.py:348
  34.9 1.5 %copy.5 = f32[12,16,128]{2,1,0:T(8,128)} copy(f32[12,16,128]{2,1,0:T(8,128)} %vcycle.1) | data formatting | bytes 196608
where the time goes:
time: 36.6 us; the launch traced here: 36.4 us
  Pallas kernels  34.9 us (95%)
  local copies, waits for them, and re-layouts  1.54 us (4%)
    pallas_call x1, Pallas kernels, body(): pl.pallas_call(functools.partial(kernel, dims), out_shape=jax.ShapeDtypeS...  34.9 us
    unnamed x1, local copies, waits for them, and re-layouts  1.54 us

commit v1 on v0

--- a/solution.py
+++ b/solution.py
@@ -347,7 +347,7 @@
     vmem = pl.BlockSpec(memory_space=pltpu.VMEM)
     return pl.pallas_call(
         functools.partial(kernel, dims),
-        out_shape=jax.ShapeDtypeStruct((X, Y, Z), f32),
+        out_shape=pltpu.VMEM((X, Y, Z), f32),
         in_specs=[pl.BlockSpec(memory_space=pl.ANY)] * 3,
         out_specs=vmem,
         scratch_shapes=[
@@ -367,8 +367,8 @@
         ]
         + [pltpu.VMEM(lead + s, f32) for lead in ((2,), (2, 3, 3)) for s in (fine, one, one, fine)]
         + [
-            pltpu.SemaphoreType.DMA((120,)),
-            pltpu.SemaphoreType.DMA((120,)),
+            pltpu.SemaphoreType.DMA((82,)),
+            pltpu.SemaphoreType.DMA((82,)),
             pltpu.SemaphoreType.DMA,
             pltpu.SemaphoreType.DMA,
             pltpu.SemaphoreType.DMA((3,)),

time: 36.6 us -> 34.4 us (0.940)
  Pallas kernels: 34.9 us -> 33.6 us
  local copies, waits for them, and re-layouts: 1.54 us -> 0.64 us
    pallas_call x1, Pallas kernels: 34.9 us -> 33.6 us  [body(): pl.pallas_call(functools.partial(kernel, dims), out_shape=pltpu.VMEM((X,...]
    unnamed x1, local copies, waits for them, and re-layouts: 1.54 us -> 0.64 us
where the time goes in v1:
time: 34.4 us; the launch traced here: 34.2 us
  Pallas kernels  33.6 us (98%)
  local copies, waits for them, and re-layouts  0.64 us (2%)
    pallas_call x1, Pallas kernels, body(): pl.pallas_call(functools.partial(kernel, dims), out_shape=pltpu.VMEM((X,...  33.6 us

profile of v1, /device:TPU:0, one launch (start us, length us, event | category | flops | bytes accessed | tf_op | source)
XLA Modules:
  0.0 34.2 jit_solution(6464886002109856852)
XLA Ops:
  0.0 33.6 %vcycle.1 = f32[12,16,128]{2,1,0:T(8,128)S(1)} custom-call(f32[12,16,128]{2,1,0:T(8,128)} %den_hbm.1, f32[12,16,128]{2,1,0:T(8,128)} %pot_hbm.1, f32[32,32]{1,0:T(8,128)} %constant.2.clone.op_hbm), custom_call_target="tpu_custom_call" | custom-call | tf_op jit(solution)/shard_map/vcycle/pallas_call | solution.py:348
  33.6 0.6 %copy.5 = f32[12,16,128]{2,1,0:T(8,128)} copy(f32[12,16,128]{2,1,0:T(8,128)S(1)} %vcycle.1) | data formatting | bytes 196608

commit v2 on v1

v2 whole, which is shorter than its diff:
```python
import functools
import numpy as np
import jax
import jax.numpy as jnp
from jax import lax
from jax.experimental import pallas as pl
from jax.experimental.pallas import tpu as pltpu
from jax.sharding import PartitionSpec as P

HI = lax.Precision.HIGHEST
MESH = pl.DeviceIdType.MESH
H, H1 = 4, 8
SIDES = ((0, 1), (0, -1), (1, 0), (-1, 0), (1, 1), (1, -1), (-1, 1), (-1, -1), (0, 0))


def table(count):
    modes = (np.arange(count) + 1) // 2
    angle = 2 * np.pi * np.outer(np.arange(count), modes) / count
    q = np.where(np.arange(count) % 2 == 1, np.cos(angle), np.sin(angle)) * np.sqrt(2 / count)
    q = np.where(2 * modes == count, np.cos(angle) / np.sqrt(count), q)
    q[:, 0] = 1 / np.sqrt(count)
    return q, 2 - 2 * np.cos(2 * np.pi * modes / count)


def coarse_operator(nx, ny, nz, wx, wy, wz):
    qx, lx = table(nx)
    qy, ly = table(ny)
    qz, lz = table(nz)
    q = np.kron(np.kron(qx, qy), qz)
    lam = wx * lx[:, None, None] + wy * ly[None, :, None] + wz * lz[None, None, :]
    lam = lam.reshape(-1)
    inv = np.concatenate([[0.0], -1.0 / lam[1:]])
    return ((q * inv) @ q.T).astype(np.float32)


def turn(v, shift):
    shift %= 128
    return pltpu.roll(v, shift, 1) if shift else v


def kernel(
    dims, den_hbm, pot_hbm, op_hbm, out_ref,
    den_v, pot_v, op_v, cp, cd, cf, cl, ce,
    z1s, z1r, zfs, zfr, zls, zlr, zes, zer,
    R, B, SR, SB, lv, ea, e2, gat, cv, dummy,
    ssem, rsem, lsem,
):
    nx, ny, nz, X, Y, Z = dims
    n = nx * ny * nz
    I, J, K = X // 2, Y // 2, Z // 2
    T, T1 = J + 2 * H, J + 2 * H1
    M = I // 2
    U = (M + 1) // 2
    G, F = X // 4, max(X // 12, 1)
    FW = X // F
    assert X % 4 == 0 and FW <= 12 and I <= 12 and 2 * K <= 128 and J % 8 == 0
    ix, iy, iz = lax.axis_index("gx"), lax.axis_index("gy"), lax.axis_index("gz")
    me = (ix * ny + iy) * nz + iz

    def around(i, count):
        return [i] + [jnp.where(i + o >= count, i + o - count, i + o) for o in range(1, count)]

    xs, ys, zs = around(ix, nx), around(iy, ny), around(iz, nz)

    def device(o):
        if isinstance(o, int):
            return (xs[o // (ny * nz)], ys[o // nz % ny], zs[o % nz])
        ox, oy, oz = o // (ny * nz), (o // nz) % ny, o % nz
        return (lax.rem(ix + ox, nx), lax.rem(iy + oy, ny), lax.rem(iz + oz, nz))

    def each_other(step):
        if n <= 64:
            for o in range(1, n):
                step(o, 0)
        else:
            lax.fori_loop(1, n, step, 0)

    wide = (lambda ref: ref) if Z == 128 else (lambda ref: ref.at[:, :, pl.ds(0, Z)])
    load_p = pltpu.make_async_copy(pot_hbm, wide(pot_v), lsem.at[0])
    load_d = pltpu.make_async_copy(den_hbm, wide(den_v), lsem.at[1])
    load_op = pltpu.make_async_copy(op_hbm, op_v, lsem.at[2])
    load_p.start()
    load_d.start()
    load_op.start()

    barrier = pltpu.get_barrier_semaphore()

    def greet(o, carry):
        pl.semaphore_signal(barrier, inc=1, device_id=device(o), device_id_type=MESH)
        return carry

    near = max(nx, ny, nz) <= 5
    steps = sorted({
        (dx % nx * ny + dy % ny) * nz + dz % nz
        for dx in (-1, 0, 1) for dy in (-1, 0, 1) for dz in (-1, 0, 1)
    } - {0})
    if near:
        for o in steps:
            greet(o, 0)
    else:
        each_other(greet)

    class Exchange:
        def __init__(self, k):
            self.k, self.rows = k, 0

        def send(self, src, dst, at, to):
            dx, dy, dz = to
            copy = pltpu.make_async_remote_copy(
                src_ref=src, dst_ref=dst, send_sem=ssem.at[self.k], recv_sem=rsem.at[self.k],
                device_id=(xs[dx], ys[dy], zs[dz]), device_id_type=MESH,
            )
            copy.start()
            self.rows += at

        def wait(self):
            all_of = dummy.at[pl.ds(0, self.rows)]
            pltpu.make_async_copy(all_of, all_of, rsem.at[self.k]).wait()
            pltpu.make_async_copy(all_of, all_of, ssem.at[self.k]).wait()

    def part(d, own, count, first):
        if d == 0:
            return first, own, first
        if d == 1:
            return first + own - count, count, first - count
        return first, count, first + own

    def block(ex, src, dst, px, py, to, shift=0, lead=None):
        (sx, cx, tx), (sy, cy, ty) = px, py
        target = dst if lead is None else dst.at[lead]
        ex.send(
            src.at[pl.ds(sx, cx), pl.ds(sy - shift, cy)],
            target.at[pl.ds(tx, cx), pl.ds(ty, cy)],
            cx * cy, to,
        )

    def iota(rows, dim):
        return lax.broadcasted_iota(jnp.int32, (rows, 128), dim)

    lane = {rows: iota(rows, 1) for rows in {J, T, T1}}

    def place(acc, v, pieces):
        by_shift = {}
        for src, dst, width in pieces:
            by_shift.setdefault((dst - src) % 128, []).append((dst, width))
        at = lane[v.shape[0]]
        for shift, spans in by_shift.items():
            mask = None
            for dst, width in spans:
                inside = (at >= dst) & (at < dst + width)
                mask = inside if mask is None else mask | inside
            moved = turn(v, shift)
            acc = jnp.where(mask, moved, acc)
        return acc

    def outside(z, right, left):
        if (right - left) % 128 == 0:
            return turn(z, right)
        return jnp.where(lane[z.shape[0]] < 96, turn(z, right), turn(z, left))

    def with_sides(v, half, z, right, left):
        own = turn(v, -K) if half else v
        if z is None:
            return own
        return jnp.where(lane[v.shape[0]] < K, own, outside(z, right, left))

    def two(a, b):
        return jnp.where(lane[a.shape[0]] < K, a, turn(b, K))

    l8 = lane[J]
    low = jnp.where(l8 < K, 2 * l8, 2 * (l8 - K) + 1) & 127
    high = jnp.where(l8 < K, 2 * l8 + 1, 2 * (l8 - K)) & 127
    order = (low, high)

    def colours(ref, x, which):
        v = [ref[x, pl.ds(b, J, stride=2), :] for b in (0, 1)]
        take = [jnp.take_along_axis(u, order[which], axis=1, mode="promise_in_bounds") for u in v]
        return jnp.where(l8 < K, take[0], take[1])

    def tile(x, t):
        forward = 0 <= x < X // 2 or x >= X
        return 2 * (x + 4) + (t if forward else 1 - t)

    load_p.wait()
    load_d.wait()
    total = jnp.zeros((J, 128), jnp.float32)
    for g in range(G):
        acc = jnp.zeros((J, 128), jnp.float32)
        for q in range(4):
            x = 4 * g + q
            black = colours(pot_v, x, 1 - x % 2)
            dens = [colours(den_v, x, x % 2), colours(den_v, x, 1 - x % 2)]
            cp[x + 5, H : H + J] = black
            acc = place(acc, black, [
                p for h in (0, 1)
                for p in ((h * K, 15 * q + 3 * h, 3), (h * K + K - 3, 61 + 15 * q + 3 * h, 3))
            ])
            for t in (0, 1):
                cd[tile(x, t), H : H + J] = dens[t]
                total = total + dens[t]
                acc = place(acc, dens[t], [
                    p for h in (0, 1) for o in (15 * q + 6 + 4 * t + 2 * h,)
                    for p in ((h * K, o, 2), (h * K + K - 2, 62 + o, 2))
                ])
        z1s[g] = acc
    total = jnp.where(l8 < 2 * K, total, 0.0)

    pl.semaphore_wait(barrier, len(steps) if near else n - 1)
    first = Exchange(0)
    for dx, dy in SIDES:
        if dx or dy:
            edge = dx != 0 and dy != 0
            block(first, cp, cp, part(dx, X, 4 if edge else 5, 5), part(dy, J, 2 if edge else 3, H), (dx, dy, 0))
            block(first, cd, cd, part(dx, 2 * X, 5 if edge else 7, 8), part(dy, J, 2, H), (dx, dy, 0))
        for dz in (1, -1):
            g0, gn, g1 = part(dx, G, 1, 1)
            block(first, z1s, z1r, (g0 - 1, gn, g1), part(dy, J, 2, H), (dx, dy, dz), H, max(dz, 0))
    first.wait()

    def base(x, b):
        return 8 + ((x + 5) * 2 + b) * T

    def get(ref, x, b, off=0):
        return ref[pl.ds(base(x, b) + off, T), :]

    def own(ref, x, b, off=0):
        return ref[pl.ds(base(x, b) + H + off, J), :]

    sides = {}

    def side(x):
        g = x // 4 + 1
        if g not in sides:
            sides[g] = jnp.where(lane[T] < 60, z1r[0, g], z1r[1, g])
        return sides[g]

    for x in range(-5, X + 5):
        far = max(-x, x - X + 1, 0)
        z = side(x) if far < 5 else None
        for h in (0, 1):
            s = 15 * (x % 4) + 3 * h
            B[pl.ds(base(x, h), T), :] = with_sides(cp[x + 5], h, z, K - s, 64 - s)
        for t, ref in ((0, SR), (1, SB)):
            if far <= 4 - t:
                for h in (0, 1):
                    s = 15 * (x % 4) + 6 + 4 * t + 2 * h
                    ref[pl.ds(base(x, h), T), :] = with_sides(cd[tile(x, t)], h, z, K - s, 64 - s)

    sixth = jnp.float32(1.0 / 6.0)

    def beside(read, v, x, b, colour):
        c = (x + b + colour) % 2
        mid = read(v, x, b)
        t = read(v, x - 1, b) + read(v, x + 1, b)
        t = t + (read(v, x, 1 - b) + read(v, x, 1 - b, 2 * b - 1))
        return t + (mid + turn(mid, 1 - 2 * c))

    def half(depth, colour):
        new, old, src = ((R, B, SR), (B, R, SB))[colour]
        for x in range(-depth, X + depth):
            for b in (0, 1):
                new[pl.ds(base(x, b), T), :] = (beside(get, old, x, b, colour) - get(src, x, b)) * sixth

    for k in range(4):
        half(4 - k, k % 2)

    def base1(p):
        return 8 + (p + 6) * T1

    def get1(ref, p, off=0):
        return ref[pl.ds(base1(p) + off, T1), :]

    one = []
    for i in range(I):
        left = None
        for x in (2 * i, 2 * i + 1):
            for b in (0, 1):
                for colour, (v, w, s) in enumerate(((R, B, SR), (B, R, SB))):
                    r = own(s, x, b) - (beside(own, w, x, b, colour) - 6.0 * own(v, x, b))
                    left = r if left is None else left + r
        one.append(left * 0.5)
    hi = 59 if 5 * I <= 59 else 64
    acc = jnp.zeros((J, 128), jnp.float32)
    for i in range(I):
        acc = place(acc, one[i], [(0, 5 * i, 5), (K - 5, hi + 5 * i, 5)])
    zls[0] = acc
    for m in range(M):
        cl[3 + m, H1 : H1 + J] = two(one[2 * m], one[2 * m + 1])

    once = nx == 2 and M == 3
    xsides = [(dx, dy) for dx, dy in SIDES if dx >= 0 or nx > 2]

    def slots(dx, single):
        if not single:
            return part(dx, 1, 1, 1)
        return (1, 1, 1) if dx == 0 else (1, 1, 0)

    second = Exchange(1)
    for dx, dy in (xsides if once else SIDES):
        px = (3, M, 0) if once and dx else part(dx, M, 3, 3)
        if dx or dy:
            block(second, cl, cl, px, part(dy, J, 4 if dx else 5, H1), (dx, dy, 0))
        if dx >= 0 or nx > 2:
            for dz in (1, -1):
                s0, sn, s1 = slots(dx, nx == 2)
                block(second, zls, zlr, (s0 - 1, sn, s1), part(dy, J, 3 if dx else 4, H1), (dx, dy, dz), H1, max(dz, 0))

    for f in range(F):
        acc = jnp.zeros((J, 128), jnp.float32)
        for q in range(FW):
            x = f * FW + q
            v = two(own(B, x, 0), own(B, x, 1))
            cf[x + 4, H : H + J] = v
            acc = place(acc, v, [
                p for h in (0, 1) for o in (4 * q + 2 * h,)
                for p in ((h * K, o, 2), (h * K + K - 2, 62 + o, 2))
            ])
        zfs[f] = acc

    second.wait()
    fourth = Exchange(3)
    for dx, dy in SIDES:
        if dx or dy:
            edge = dx != 0 and dy != 0
            block(fourth, cf, cf, part(dx, X, 3 if edge else 4, 4), part(dy, J, 2, H), (dx, dy, 0))
        for dz in (1, -1):
            g0, gn, g1 = part(dx, F, 1, 1)
            block(fourth, zfs, zfr, (g0 - 1, gn, g1), part(dy, J, 2, H), (dx, dy, dz), H, max(dz, 0))

    def slot_of(p, count):
        if p < 0:
            return 0, p + count
        if p >= count:
            return (0 if nx == 2 else 2), p - count
        return 1, p

    zl = [jnp.where(lane[T1] < hi, zlr[0, s], zlr[1, s]) for s in range(2 if nx == 2 else 3)]
    for p in range(-5, I + 5):
        slot, i = slot_of(p, I)
        m = i // 2
        at = 3 + m if slot == 1 else (m - (M - 3) if p < 0 or once else 3 + M + m)
        lv[pl.ds(base1(p), T1), :] = with_sides(cl[at], i % 2, zl[slot], K - 5 * i, 123 - hi - 5 * i)

    even = (iota(T1, 0) + lane[T1]) % 2 == 0
    mask = (even, jnp.logical_not(even))

    def beside1(read, v, p, c):
        t = read(v, p - 1) + read(v, p + 1)
        t = t + (read(v, p, -1) + read(v, p, 1))
        return t + (turn(c, 1) + turn(c, -1))

    def half1(depth, colour, shift=None, read=get1, src=ea):
        for p in range(-depth, I + depth):
            c = read(src, p)
            t = beside1(read, src, p, c) - get1(lv, p)
            if shift is not None:
                t = t + shift
            ea[pl.ds(base1(p), T1), :] = jnp.where(mask[(p + colour) % 2], t * sixth, c)

    for p in range(-4, I + 4):
        ea[pl.ds(base1(p), T1), :] = jnp.where(mask[p % 2], get1(lv, p) * -sixth, 0.0)
    for depth, colour in ((3, 1), (2, 0), (1, 1)):
        half1(depth, colour)

    def own1(ref, p, off=0):
        return ref[pl.ds(base1(p) + H1 + off, J), :]

    acc = jnp.zeros((J, 128), jnp.float32)
    for p in range(I):
        c = own1(ea, p)
        acc = acc + (own1(lv, p) - (beside1(own1, ea, p, c) - 6.0 * c))
    acc = jnp.where(l8 < K, acc, 0.0)

    def whole_sum(v):
        return jnp.sum(jnp.sum(v, axis=0, keepdims=True), axis=1, keepdims=True)

    lane1 = lax.broadcasted_iota(jnp.int32, (1, 128), 1)
    gat[me] = jnp.where(lane1 < 64, whole_sum(acc), whole_sum(total))

    def spread(o, carry):
        pltpu.make_async_remote_copy(
            src_ref=gat.at[me], dst_ref=gat.at[me], send_sem=ssem.at[4], recv_sem=rsem.at[4],
            device_id=device(o), device_id_type=MESH,
        ).start()
        return carry

    each_other(spread)

    odd = (iota(J, 0) + l8) % 2 == 1
    black = [jnp.where(odd, own1(ea, 2 * m), own1(ea, 2 * m + 1)) for m in range(M)]
    acc = jnp.zeros((J, 128), jnp.float32)
    for m in range(M):
        acc = place(acc, black[m], [(0, 6 * m, 6), (K - 6, 58 + 6 * m, 6)])
    zes[0] = acc
    for u in range(U):
        ce[2 + u, H1 : H1 + J] = two(black[2 * u], black[2 * u + 1]) if 2 * u + 1 < M else black[2 * u]
    third = Exchange(2)
    once3 = nx == 2 and U == 2
    for dx, dy in (xsides if once3 else SIDES):
        px = (2, U, 0) if once3 and dx else part(dx, U, 2, 2)
        if dx or dy:
            block(third, ce, ce, px, part(dy, J, 5 if dx else 6, H1), (dx, dy, 0))
        if dx >= 0 or nx > 2:
            for dz in (1, -1):
                s0, sn, s1 = slots(dx, nx == 2)
                block(third, zes, zer, (s0 - 1, sn, s1), part(dy, J, 4 if dx else 5, H1), (dx, dy, dz), H1, max(dz, 0))

    fourth.wait()
    for x in range(-4, X + 4):
        far = max(-x, x - X + 1, 0)
        z = None
        if far < 4:
            f = 0 if x < 0 else (F + 1 if x >= X else x // FW + 1)
            if ("f", f) not in sides:
                sides["f", f] = jnp.where(lane[T] < 60, zfr[0, f], zfr[1, f])
            z = sides["f", f]
        for h in (0, 1):
            s = 4 * (x % FW) + 2 * h
            B[pl.ds(base(x, h), T), :] = with_sides(cf[x + 4], h, z, K - s, 64 - s)

    third.wait()
    others = gat.at[pl.ds(0, n - 1)]
    pltpu.make_async_copy(others, others, ssem.at[4]).wait()
    pltpu.make_async_copy(others, others, rsem.at[4]).wait()
    load_op.wait()
    values = gat[:, 0, :]
    swapped = pltpu.roll(values, 64, 1)
    below = lax.broadcasted_iota(jnp.int32, (n, 128), 1) < 64
    blocks = jnp.where(below, values, swapped)
    mean = jnp.sum(jnp.where(below, swapped, values), axis=0, keepdims=True) / jnp.float32(n * X * Y * Z)
    blocks = blocks - jnp.sum(blocks, axis=0, keepdims=True) / jnp.float32(n)
    cv[...] = jnp.dot(op_v[...], blocks, precision=HI, preferred_element_type=jnp.float32)
    row = iota(T1, 0)
    at = lane[T1]
    maps = []
    for dx in (-1, 0, 1):
        by_row = []
        for dy in (-1, 0, 1):
            vals = []
            for dz in (-1, 0, 1):
                o = (xs[dx] * ny + ys[dy]) * nz
                vals.append(cv[pl.ds(o + zs[dz], 1), :])
            by_row.append(jnp.where(at < K, vals[1], jnp.where(at < (K + 128) // 2, vals[2], vals[0])))
        field = jnp.where(row < H1, by_row[0], jnp.where(row < H1 + J, by_row[1], by_row[2]))
        maps.append(field + mean * jnp.float32(8.0 / 3.0))

    def base2(m):
        return 8 + (m + 3) * T1

    ze = [jnp.where(lane[T1] < 58, zer[0, s], zer[1, s]) for s in range(2 if nx == 2 else 3)]
    for mm in range(-3, M + 3):
        slot, m = slot_of(mm, M)
        u = m // 2
        at = 2 + u if slot == 1 else (u - (U - 2) if mm < 0 or once3 else 2 + U + u)
        v = with_sides(ce[at], m % 2, ze[slot], K - 6 * m, 64 - 6 * m)
        e2[pl.ds(base2(mm), T1), :] = v + maps[0 if mm < 0 else (1 if mm < M else 2)]

    def get2(ref, p, off=0):
        return ref[pl.ds(base2(p // 2) + off, T1), :]

    shift = 4.0 * mean
    half1(5, 0, shift, get2, e2)
    for depth, colour in ((4, 1), (3, 0), (2, 1)):
        half1(depth, colour, shift)

    rise = mean * jnp.float32(2.0 / 3.0)
    for i in range(-2, I + 2):
        e = ea[pl.ds(base1(i) + H1 - H, T), :] + rise
        for x in (2 * i, 2 * i + 1):
            for b in (0, 1):
                B[pl.ds(base(x, b), T), :] = get(B, x, b) + e

    def last(depth, colour):
        new, old, src = ((R, B, SR), (B, R, SB))[colour]
        for x in range(-depth, X + depth):
            for b in (0, 1):
                t = beside(get, old, x, b, colour) - get(src, x, b) + mean
                new[pl.ds(base(x, b), T), :] = t * sixth

    last(3, 0)
    last(2, 1)
    last(1, 0)
    back = l8 >> 1
    odd_lane = (l8 & 1) == 1
    for x in range(X):
        for b in (0, 1):
            red = own(R, x, b)
            dark = (beside(own, R, x, b, 1) - own(SB, x, b) + mean) * sixth
            pair = (red, dark) if (x + b) % 2 == 0 else (dark, red)
            e, o = (jnp.take_along_axis(v, back, axis=1, mode="promise_in_bounds") for v in pair)
            out_ref[x, pl.ds(b, J, stride=2), :] = jnp.where(odd_lane, o, e)[:, 0:Z]


def body(dims, density, potential):
    nx, ny, nz, X, Y, Z = dims
    n = nx * ny * nz
    I, J, K = X // 2, Y // 2, Z // 2
    T, T1 = J + 2 * H, J + 2 * H1
    M = I // 2
    U = (M + 1) // 2
    G, F = X // 4, max(X // 12, 1)
    op = coarse_operator(nx, ny, nz, float(J * K), float(I * K), float(I * J))
    fine = 16 + (X + 10) * 2 * T
    coarse = 16 + (I + 12) * T1

    def vmem(*shape):
        return pltpu.VMEM(shape, jnp.float32)

    return pl.pallas_call(
        functools.partial(kernel, dims),
        out_shape=pltpu.VMEM((X, Y, Z), jnp.float32),
        in_specs=[pl.BlockSpec(memory_space=pl.ANY)] * 3,
        out_specs=pl.BlockSpec(memory_space=pltpu.VMEM),
        scratch_shapes=[
            vmem(X, Y, 128),
            vmem(X, Y, 128),
            vmem(n, n),
            vmem(X + 10, T, 128),
            vmem(2 * (X + 8), T, 128),
            vmem(X + 8, T, 128),
            vmem(M + 6, T1, 128),
            vmem(U + 4, T1, 128),
            vmem(G, J, 128),
            vmem(2, G + 2, T, 128),
            vmem(F, J, 128),
            vmem(2, F + 2, T, 128),
            vmem(1, J, 128),
            vmem(2, 3, T1, 128),
            vmem(1, J, 128),
            vmem(2, 3, T1, 128),
            vmem(fine, 128),
            vmem(fine, 128),
            vmem(fine, 128),
            vmem(fine, 128),
            vmem(coarse, 128),
            vmem(coarse, 128),
            vmem(16 + (M + 6) * T1, 128),
            vmem(n, 1, 128),
            vmem(n, 128),
            vmem(2048, 128),
            pltpu.SemaphoreType.DMA((5,)),
            pltpu.SemaphoreType.DMA((5,)),
            pltpu.SemaphoreType.DMA((3,)),
        ],
        compiler_params=pltpu.CompilerParams(collective_id=0, has_side_effects=True),
        name="vcycle",
    )(density, potential, op)


def solution(mesh):
    nx, ny, nz = (mesh.shape[a] for a in ("gx", "gy", "gz"))

    def run(density, potential):
        return body((nx, ny, nz) + density.shape, density, potential)

    spec = P("gx", "gy", "gz")
    return jax.shard_map(run, mesh=mesh, in_specs=(spec, spec), out_specs=spec, check_vma=False)
```

time: 34.4 us -> 24.9 us (0.72)
  Pallas kernels: 33.6 us -> 24.1 us
    pallas_call x1, Pallas kernels: 33.6 us -> 24.1 us  [body(): pl.pallas_call(functools.partial(kernel, dims), out_shape=pltpu.VMEM((X,...]
where the time goes in v2:
time: 24.9 us; the launch traced here: 24.7 us
  Pallas kernels  24.1 us (97%)
  local copies, waits for them, and re-layouts  0.64 us (3%)
    pallas_call x1, Pallas kernels, body(): pl.pallas_call(functools.partial(kernel, dims), out_shape=pltpu.VMEM((X,...  24.1 us
    unnamed x1, local copies, waits for them, and re-layouts  0.64 us

profile of v2, /device:TPU:0, one launch (start us, length us, event | category | flops | bytes accessed | tf_op | source)
XLA Modules:
  0.0 24.7 jit_solution(9163871075936591946)
XLA Ops:
  0.0 24.1 %vcycle.1 = f32[12,16,128]{2,1,0:T(8,128)S(1)} custom-call(f32[12,16,128]{2,1,0:T(8,128)} %den_hbm.1, f32[12,16,128]{2,1,0:T(8,128)} %pot_hbm.1, f32[32,32]{1,0:T(8,128)} %constant.2.clone.op_hbm), custom_call_target="tpu_custom_call" | custom-call | tf_op jit(solution)/shard_map/vcycle/pallas_call | solution.py:509
  24.1 0.6 %copy.5 = f32[12,16,128]{2,1,0:T(8,128)} copy(f32[12,16,128]{2,1,0:T(8,128)S(1)} %vcycle.1) | data formatting | bytes 196608

commit v3 on v2

--- a/solution.py
+++ b/solution.py
@@ -9,8 +9,9 @@
 
 HI = lax.Precision.HIGHEST
 MESH = pl.DeviceIdType.MESH
-H, H1 = 4, 8
-SIDES = ((0, 1), (0, -1), (1, 0), (-1, 0), (1, 1), (1, -1), (-1, 1), (-1, -1), (0, 0))
+H, H1 = 4, 12
+DEEP = 9
+SIDES = ((1, 1), (1, -1), (-1, 1), (-1, -1), (0, 1), (0, -1), (0, 0), (1, 0), (-1, 0))
 
 
 def table(count):
@@ -33,16 +34,61 @@
     return ((q * inv) @ q.T).astype(np.float32)
 
 
+def offsets(nx, ny, nz):
+    steps = [(dx % nx, dy % ny, dz % nz) for dx in (0, 1, -1) for dy in (0, 1, -1) for dz in (0, 1, -1)]
+    return list(dict.fromkeys(steps))
+
+
+def residual_weights(nx, ny, nz, I, J, K):
+    block = np.zeros((3 * I, 3 * J, 3 * K))
+    block[I : 2 * I, J : 2 * J, K : 2 * K] = 1.0
+
+    def beside(v):
+        return sum(np.roll(v, d, axis) for axis in range(3) for d in (1, -1))
+
+    red = np.indices(block.shape).sum(0) % 2 == 0
+    v = beside(block) - 6.0 * block
+    black2 = np.where(red, 0.0, v)
+    red2 = np.where(red, v + beside(black2) / 6.0, 0.0)
+    black1 = np.where(red, 0.0, beside(red2) / 6.0)
+    red1 = np.where(red, beside(black1) / 6.0, 0.0)
+    w = block + (black2 + red2 + black1 + red1) / 6.0
+    names = offsets(nx, ny, nz)
+    own = np.zeros((len(names), I, J, K))
+    for dx in (0, 1, -1):
+        for dy in (0, 1, -1):
+            for dz in (0, 1, -1):
+                x, y, z = (1 - dx) * I, (1 - dy) * J, (1 - dz) * K
+                own[names.index((dx % nx, dy % ny, dz % nz))] += w[x : x + I, y : y + J, z : z + K]
+    even = np.indices((J, K)).sum(0) % 2 == 0
+    first, second = own[:, 0::2], own[:, 1::2]
+    out = np.zeros((len(names), I // 2, J, 128))
+    out[..., :K] = np.where(even, first, second)
+    out[..., K : 2 * K] = np.where(even, second, first)
+    return out.astype(np.float32)
+
+
+def coarse_weights(op, nx, ny, nz):
+    names = offsets(nx, ny, nz)
+    green = op.astype(np.float64)[:, 0].reshape(nx, ny, nz)
+    rx, ry, rz = np.indices((nx, ny, nz)).reshape(3, -1)
+    out = np.zeros((len(names), nx * ny * nz, 128))
+    for o, (ox, oy, oz) in enumerate(names):
+        for f, (fx, fy, fz) in enumerate(names):
+            out[o, :, f] = green[(ox - rx - fx) % nx, (oy - ry - fy) % ny, (oz - rz - fz) % nz]
+    return out.astype(np.float32)
+
+
 def turn(v, shift):
     shift %= 128
     return pltpu.roll(v, shift, 1) if shift else v
 
 
 def kernel(
-    dims, den_hbm, pot_hbm, op_hbm, out_ref,
-    den_v, pot_v, op_v, cp, cd, cf, cl, ce,
-    z1s, z1r, zfs, zfr, zls, zlr, zes, zer,
-    R, B, SR, SB, lv, ea, e2, gat, cv, dummy,
+    dims, den_hbm, pot_hbm, rw_hbm, cw_hbm, out_ref,
+    den_v, pot_v, rw, cw, cp, cd, cf, cl,
+    z1s, z1r, zfs, zfr, zls, zlr,
+    R, B, SR, SB, LR, LB, ER, EB, gat, cv, dummy,
     ssem, rsem, lsem,
 ):
     nx, ny, nz, X, Y, Z = dims
@@ -50,10 +96,14 @@
     I, J, K = X // 2, Y // 2, Z // 2
     T, T1 = J + 2 * H, J + 2 * H1
     M = I // 2
-    U = (M + 1) // 2
-    G, F = X // 4, max(X // 12, 1)
+    ring = nx == 2 and I < DEEP
+    E = 0 if ring else 5
+    G, F, GL = X // 4, max(X // 12, 1), M // 3
     FW = X // F
-    assert X % 4 == 0 and FW <= 12 and I <= 12 and 2 * K <= 128 and J % 8 == 0
+    assert X % 12 == 0 and FW <= 12 and 2 * K <= 128 and J % 8 == 0 and 2 * J > DEEP and 2 * M >= E and M % 3 == 0
+    names = offsets(nx, ny, nz)
+    NF = len(names)
+    Q = -(-(NF + 1) // 8) * 8
     ix, iy, iz = lax.axis_index("gx"), lax.axis_index("gy"), lax.axis_index("gz")
     me = (ix * ny + iy) * nz + iz
 
@@ -78,10 +128,12 @@
     wide = (lambda ref: ref) if Z == 128 else (lambda ref: ref.at[:, :, pl.ds(0, Z)])
     load_p = pltpu.make_async_copy(pot_hbm, wide(pot_v), lsem.at[0])
     load_d = pltpu.make_async_copy(den_hbm, wide(den_v), lsem.at[1])
-    load_op = pltpu.make_async_copy(op_hbm, op_v, lsem.at[2])
+    load_rw = pltpu.make_async_copy(rw_hbm, rw, lsem.at[2])
+    load_cw = pltpu.make_async_copy(cw_hbm, cw, lsem.at[3])
     load_p.start()
     load_d.start()
-    load_op.start()
+    load_rw.start()
+    load_cw.start()
 
     barrier = pltpu.get_barrier_semaphore()
 
@@ -264,12 +316,10 @@
     for k in range(4):
         half(4 - k, k % 2)
 
-    def base1(p):
-        return 8 + (p + 6) * T1
-
-    def get1(ref, p, off=0):
-        return ref[pl.ds(base1(p) + off, T1), :]
-
+    def even_at(rows):
+        return (iota(rows, 0) + lane[rows]) % 2 == 0
+
+    even = {rows: even_at(rows) for rows in {J, T}}
     one = []
     for i in range(I):
         left = None
@@ -279,31 +329,66 @@
                     r = own(s, x, b) - (beside(own, w, x, b, colour) - 6.0 * own(v, x, b))
                     left = r if left is None else left + r
         one.append(left * 0.5)
-    hi = 59 if 5 * I <= 59 else 64
-    acc = jnp.zeros((J, 128), jnp.float32)
-    for i in range(I):
-        acc = place(acc, one[i], [(0, 5 * i, 5), (K - 5, hi + 5 * i, 5)])
-    zls[0] = acc
-    for m in range(M):
-        cl[3 + m, H1 : H1 + J] = two(one[2 * m], one[2 * m + 1])
-
-    once = nx == 2 and M == 3
-    xsides = [(dx, dy) for dx, dy in SIDES if dx >= 0 or nx > 2]
-
-    def slots(dx, single):
-        if not single:
-            return part(dx, 1, 1, 1)
-        return (1, 1, 1) if dx == 0 else (1, 1, 0)
+    load_rw.wait()
+    sums = [jnp.zeros((J, 128), jnp.float32) for _ in names]
+    for g in range(GL):
+        acc = jnp.zeros((J, 128), jnp.float32)
+        for q in range(3):
+            m = 3 * g + q
+            red = jnp.where(even[J], one[2 * m], one[2 * m + 1])
+            black = jnp.where(even[J], one[2 * m + 1], one[2 * m])
+            both = two(red, black)
+            if 2 * K < 128:
+                both = jnp.where(l8 < 2 * K, both, 0.0)
+            cl[E + m, H1 : H1 + J] = both
+            sums = [a + rw[f, m] * both for f, a in enumerate(sums)]
+            for c, v in enumerate((red, black)):
+                s = 18 * q + 9 * c
+                acc = place(acc, v, [(0, s, DEEP), (K - DEEP, 55 + s, DEEP)])
+        zls[g] = acc
+
+    def stack(rows):
+        rows = [jnp.sum(v, axis=0, keepdims=True) for v in rows]
+        rows = rows + [jnp.zeros((1, 128), jnp.float32)] * (Q - len(rows))
+        return jnp.sum(jnp.concatenate(rows, axis=0), axis=1, keepdims=True)
+
+    spot = lax.broadcasted_iota(jnp.int32, (Q, 128), 0) == lax.broadcasted_iota(jnp.int32, (Q, 128), 1)
+    gat[0] = jnp.sum(jnp.where(spot, stack(sums + [total]), 0.0), axis=0, keepdims=True)
+
+    def spread(o, carry):
+        if isinstance(o, int):
+            there = ((-(o // (ny * nz)) % nx) * ny + -(o // nz) % ny) * nz + -o % nz
+        else:
+            ox, oy, oz = o // (ny * nz), (o // nz) % ny, o % nz
+            there = (lax.rem(nx - ox, nx) * ny + lax.rem(ny - oy, ny)) * nz + lax.rem(nz - oz, nz)
+        pltpu.make_async_remote_copy(
+            src_ref=gat.at[0], dst_ref=gat.at[there], send_sem=ssem.at[2], recv_sem=rsem.at[2],
+            device_id=device(o), device_id_type=MESH,
+        ).start()
+        return carry
+
+    each_other(spread)
 
     second = Exchange(1)
-    for dx, dy in (xsides if once else SIDES):
-        px = (3, M, 0) if once and dx else part(dx, M, 3, 3)
-        if dx or dy:
-            block(second, cl, cl, px, part(dy, J, 4 if dx else 5, H1), (dx, dy, 0))
-        if dx >= 0 or nx > 2:
+
+    def deep(d, own, count, first):
+        if abs(d) < 2:
+            return part(d, own, min(own, count), first)
+        count -= own
+        return (first + own - count, count, first - own - count) if d > 0 else (first, count, first + 2 * own)
+
+    ways = (2, -2, 1, -1, 0)
+    for dy in ways:
+        for dx in (1, 0) if ring else ways:
+            if abs(dx) + abs(dy) > 3 or (abs(dy) == 2 and J >= DEEP) or (abs(dx) == 2 and M >= E):
+                continue
+            px = (0, M, M if dx else 0) if ring else deep(dx, M, E, E)
+            pz = (0, GL, GL * dx) if ring else (0, GL, GL * (2 - dx))
+            py = deep(dy, J, DEEP, H1)
             for dz in (1, -1):
-                s0, sn, s1 = slots(dx, nx == 2)
-                block(second, zls, zlr, (s0 - 1, sn, s1), part(dy, J, 3 if dx else 4, H1), (dx, dy, dz), H1, max(dz, 0))
+                block(second, zls, zlr, pz, py, (dx, dy, dz), H1, max(dz, 0))
+            if dx or dy:
+                block(second, cl, cl, px, py, (dx, dy, 0))
 
     for f in range(F):
         acc = jnp.zeros((J, 128), jnp.float32)
@@ -316,8 +401,6 @@
                 for p in ((h * K, o, 2), (h * K + K - 2, 62 + o, 2))
             ])
         zfs[f] = acc
-
-    second.wait()
     fourth = Exchange(3)
     for dx, dy in SIDES:
         if dx or dy:
@@ -327,148 +410,109 @@
             g0, gn, g1 = part(dx, F, 1, 1)
             block(fourth, zfs, zfr, (g0 - 1, gn, g1), part(dy, J, 2, H), (dx, dy, dz), H, max(dz, 0))
 
-    def slot_of(p, count):
-        if p < 0:
-            return 0, p + count
-        if p >= count:
-            return (0 if nx == 2 else 2), p - count
-        return 1, p
-
-    zl = [jnp.where(lane[T1] < hi, zlr[0, s], zlr[1, s]) for s in range(2 if nx == 2 else 3)]
-    for p in range(-5, I + 5):
-        slot, i = slot_of(p, I)
-        m = i // 2
-        at = 3 + m if slot == 1 else (m - (M - 3) if p < 0 or once else 3 + M + m)
-        lv[pl.ds(base1(p), T1), :] = with_sides(cl[at], i % 2, zl[slot], K - 5 * i, 123 - hi - 5 * i)
-
-    even = (iota(T1, 0) + lane[T1]) % 2 == 0
-    mask = (even, jnp.logical_not(even))
-
-    def beside1(read, v, p, c):
-        t = read(v, p - 1) + read(v, p + 1)
-        t = t + (read(v, p, -1) + read(v, p, 1))
-        return t + (turn(c, 1) + turn(c, -1))
-
-    def half1(depth, colour, shift=None, read=get1, src=ea):
-        for p in range(-depth, I + depth):
-            c = read(src, p)
-            t = beside1(read, src, p, c) - get1(lv, p)
+    load_cw.wait()
+    others = gat.at[pl.ds(0, n - 1)]
+    pltpu.make_async_copy(others, others, rsem.at[2]).wait()
+    pltpu.make_async_copy(others, others, ssem.at[2]).wait()
+    values = gat[:, 0, :]
+    whole = jnp.sum(values, axis=0, keepdims=True)
+    values = values - whole / jnp.float32(n)
+    lane1 = lax.broadcasted_iota(jnp.int32, (1, 128), 1)
+    cv[...] = jnp.broadcast_to(
+        stack([cw[o] * values for o in range(NF)] + [jnp.where(lane1 == NF, whole, 0.0)]), (Q, 128)
+    )
+    mean = cv[NF : NF + 1, :] / jnp.float32(n * X * Y * Z)
+    row = iota(T1, 0)
+    at = lane[T1]
+    maps = {}
+    for dx in ((0, 1) if ring else (0, 1, -1)):
+        by_row = []
+        for dy in (-1, 0, 1):
+            vals = [cv[names.index((dx % nx, dy % ny, dz % nz)), :][None] for dz in (-1, 0, 1)]
+            by_row.append(jnp.where(at < K, vals[1], jnp.where(at < (K + 128) // 2, vals[2], vals[0])))
+        field = jnp.where(row < H1, by_row[0], jnp.where(row < H1 + J, by_row[1], by_row[2]))
+        maps[dx] = field + mean * jnp.float32(8.0 / 3.0)
+
+    def base1(m):
+        return 8 + ((m % (2 * M)) if ring else m + 6) * T1
+
+    def span(depth):
+        low, high = (-depth) // 2, (I - 1 + depth) // 2
+        return range(2 * M) if ring and high - low + 1 >= 2 * M else range(low, high + 1)
+
+    def window(depth):
+        reach = -(-depth // 4) * 4
+        return H1 - reach, J + 2 * reach
+
+    def get1(ref, m, start, rows):
+        return ref[pl.ds(base1(m) + start, rows), :]
+
+    second.wait()
+    sides.clear()
+    for m in span(DEEP):
+        g, q = m // 3 + (0 if ring else 2 * GL), m % 3
+        if g not in sides:
+            sides[g] = jnp.where(lane[T1] < 55, zlr[0, g], zlr[1, g])
+        for c, ref in ((0, LR), (1, LB)):
+            s = 18 * q + 9 * c
+            ref[pl.ds(base1(m), T1), :] = with_sides(cl[m + E], c, sides[g], K - s, 64 - s)
+
+    for m in span(DEEP):
+        ER[pl.ds(base1(m), T1), :] = get1(LR, m, 0, T1) * -sixth
+
+    masks = {}
+
+    def even_from(start, rows):
+        if rows not in masks:
+            masks[rows] = (lax.broadcasted_iota(jnp.int32, (rows, 128), 0) + lax.broadcasted_iota(jnp.int32, (rows, 128), 1)) % 2 == 0
+        return masks[rows] if start % 2 == 0 else jnp.logical_not(masks[rows])
+
+    def half1(depth, colour, shift=None, first=False):
+        new, old, src = ((ER, EB, LR), (EB, ER, LB))[colour]
+        start, rows = window(depth)
+        mask = even_from(start, rows)
+        for m in span(depth):
+            c = get1(old, m, start, rows)
+            before, after = get1(old, m - 1, start, rows), get1(old, m + 1, start, rows)
+            t = c + (jnp.where(mask, before, after) if colour == 0 else jnp.where(mask, after, before))
+            t = t + (get1(old, m, start - 1, rows) + get1(old, m, start + 1, rows))
+            t = t + (turn(c, 1) + turn(c, -1)) - get1(src, m, start, rows)
             if shift is not None:
                 t = t + shift
-            ea[pl.ds(base1(p), T1), :] = jnp.where(mask[(p + colour) % 2], t * sixth, c)
-
-    for p in range(-4, I + 4):
-        ea[pl.ds(base1(p), T1), :] = jnp.where(mask[p % 2], get1(lv, p) * -sixth, 0.0)
-    for depth, colour in ((3, 1), (2, 0), (1, 1)):
-        half1(depth, colour)
-
-    def own1(ref, p, off=0):
-        return ref[pl.ds(base1(p) + H1 + off, J), :]
-
-    acc = jnp.zeros((J, 128), jnp.float32)
-    for p in range(I):
-        c = own1(ea, p)
-        acc = acc + (own1(lv, p) - (beside1(own1, ea, p, c) - 6.0 * c))
-    acc = jnp.where(l8 < K, acc, 0.0)
-
-    def whole_sum(v):
-        return jnp.sum(jnp.sum(v, axis=0, keepdims=True), axis=1, keepdims=True)
-
-    lane1 = lax.broadcasted_iota(jnp.int32, (1, 128), 1)
-    gat[me] = jnp.where(lane1 < 64, whole_sum(acc), whole_sum(total))
-
-    def spread(o, carry):
-        pltpu.make_async_remote_copy(
-            src_ref=gat.at[me], dst_ref=gat.at[me], send_sem=ssem.at[4], recv_sem=rsem.at[4],
-            device_id=device(o), device_id_type=MESH,
-        ).start()
-        return carry
-
-    each_other(spread)
-
-    odd = (iota(J, 0) + l8) % 2 == 1
-    black = [jnp.where(odd, own1(ea, 2 * m), own1(ea, 2 * m + 1)) for m in range(M)]
-    acc = jnp.zeros((J, 128), jnp.float32)
-    for m in range(M):
-        acc = place(acc, black[m], [(0, 6 * m, 6), (K - 6, 58 + 6 * m, 6)])
-    zes[0] = acc
-    for u in range(U):
-        ce[2 + u, H1 : H1 + J] = two(black[2 * u], black[2 * u + 1]) if 2 * u + 1 < M else black[2 * u]
-    third = Exchange(2)
-    once3 = nx == 2 and U == 2
-    for dx, dy in (xsides if once3 else SIDES):
-        px = (2, U, 0) if once3 and dx else part(dx, U, 2, 2)
-        if dx or dy:
-            block(third, ce, ce, px, part(dy, J, 5 if dx else 6, H1), (dx, dy, 0))
-        if dx >= 0 or nx > 2:
-            for dz in (1, -1):
-                s0, sn, s1 = slots(dx, nx == 2)
-                block(third, zes, zer, (s0 - 1, sn, s1), part(dy, J, 4 if dx else 5, H1), (dx, dy, dz), H1, max(dz, 0))
+            new[pl.ds(base1(m) + start, rows), :] = t * sixth
+
+    half1(8, 1)
+    half1(7, 0)
+    half1(6, 1)
+    for m in span(6):
+        dx = (0 if 0 <= m < M else 1) if ring else (-1 if m < 0 else (0 if m < M else 1))
+        start, rows = window(6)
+        EB[pl.ds(base1(m) + start, rows), :] = get1(EB, m, start, rows) + maps[dx][start : start + rows]
+    shift = 4.0 * mean
+    half1(5, 0, shift)
+    half1(4, 1, shift)
+    half1(3, 0, shift)
+    half1(2, 1, shift)
 
     fourth.wait()
-    for x in range(-4, X + 4):
-        far = max(-x, x - X + 1, 0)
-        z = None
-        if far < 4:
-            f = 0 if x < 0 else (F + 1 if x >= X else x // FW + 1)
-            if ("f", f) not in sides:
-                sides["f", f] = jnp.where(lane[T] < 60, zfr[0, f], zfr[1, f])
-            z = sides["f", f]
-        for h in (0, 1):
-            s = 4 * (x % FW) + 2 * h
-            B[pl.ds(base(x, h), T), :] = with_sides(cf[x + 4], h, z, K - s, 64 - s)
-
-    third.wait()
-    others = gat.at[pl.ds(0, n - 1)]
-    pltpu.make_async_copy(others, others, ssem.at[4]).wait()
-    pltpu.make_async_copy(others, others, rsem.at[4]).wait()
-    load_op.wait()
-    values = gat[:, 0, :]
-    swapped = pltpu.roll(values, 64, 1)
-    below = lax.broadcasted_iota(jnp.int32, (n, 128), 1) < 64
-    blocks = jnp.where(below, values, swapped)
-    mean = jnp.sum(jnp.where(below, swapped, values), axis=0, keepdims=True) / jnp.float32(n * X * Y * Z)
-    blocks = blocks - jnp.sum(blocks, axis=0, keepdims=True) / jnp.float32(n)
-    cv[...] = jnp.dot(op_v[...], blocks, precision=HI, preferred_element_type=jnp.float32)
-    row = iota(T1, 0)
-    at = lane[T1]
-    maps = []
-    for dx in (-1, 0, 1):
-        by_row = []
-        for dy in (-1, 0, 1):
-            vals = []
-            for dz in (-1, 0, 1):
-                o = (xs[dx] * ny + ys[dy]) * nz
-                vals.append(cv[pl.ds(o + zs[dz], 1), :])
-            by_row.append(jnp.where(at < K, vals[1], jnp.where(at < (K + 128) // 2, vals[2], vals[0])))
-        field = jnp.where(row < H1, by_row[0], jnp.where(row < H1 + J, by_row[1], by_row[2]))
-        maps.append(field + mean * jnp.float32(8.0 / 3.0))
-
-    def base2(m):
-        return 8 + (m + 3) * T1
-
-    ze = [jnp.where(lane[T1] < 58, zer[0, s], zer[1, s]) for s in range(2 if nx == 2 else 3)]
-    for mm in range(-3, M + 3):
-        slot, m = slot_of(mm, M)
-        u = m // 2
-        at = 2 + u if slot == 1 else (u - (U - 2) if mm < 0 or once3 else 2 + U + u)
-        v = with_sides(ce[at], m % 2, ze[slot], K - 6 * m, 64 - 6 * m)
-        e2[pl.ds(base2(mm), T1), :] = v + maps[0 if mm < 0 else (1 if mm < M else 2)]
-
-    def get2(ref, p, off=0):
-        return ref[pl.ds(base2(p // 2) + off, T1), :]
-
-    shift = 4.0 * mean
-    half1(5, 0, shift, get2, e2)
-    for depth, colour in ((4, 1), (3, 0), (2, 1)):
-        half1(depth, colour, shift)
-
+    sides.clear()
     rise = mean * jnp.float32(2.0 / 3.0)
-    for i in range(-2, I + 2):
-        e = ea[pl.ds(base1(i) + H1 - H, T), :] + rise
-        for x in (2 * i, 2 * i + 1):
-            for b in (0, 1):
-                B[pl.ds(base(x, b), T), :] = get(B, x, b) + e
+    for m in range(-1, M + 1):
+        tiles = [get1(v, m, H1 - H, T) for v in (ER, EB)]
+        for i in (2 * m, 2 * m + 1):
+            first_, second_ = tiles if i % 2 == 0 else tiles[::-1]
+            e = jnp.where(even[T], first_, second_) + rise
+            for x in (2 * i, 2 * i + 1):
+                far = max(-x, x - X + 1, 0)
+                z = None
+                if far < 4:
+                    f = 0 if x < 0 else (F + 1 if x >= X else x // FW + 1)
+                    if f not in sides:
+                        sides[f] = jnp.where(lane[T] < 60, zfr[0, f], zfr[1, f])
+                    z = sides[f]
+                for h in (0, 1):
+                    s = 4 * (x % FW) + 2 * h
+                    B[pl.ds(base(x, h), T), :] = with_sides(cf[x + 4], h, z, K - s, 64 - s) + e
 
     def last(depth, colour):
         new, old, src = ((R, B, SR), (B, R, SB))[colour]
@@ -497,11 +541,14 @@
     I, J, K = X // 2, Y // 2, Z // 2
     T, T1 = J + 2 * H, J + 2 * H1
     M = I // 2
-    U = (M + 1) // 2
-    G, F = X // 4, max(X // 12, 1)
+    ring = nx == 2 and I < DEEP
+    G, F, GL = X // 4, max(X // 12, 1), M // 3
     op = coarse_operator(nx, ny, nz, float(J * K), float(I * K), float(I * J))
+    rw = residual_weights(nx, ny, nz, I, J, K)
+    cw = coarse_weights(op, nx, ny, nz)
+    Q = -(-(len(rw) + 1) // 8) * 8
     fine = 16 + (X + 10) * 2 * T
-    coarse = 16 + (I + 12) * T1
+    coarse = 16 + (2 * M if ring else M + 12) * T1
 
     def vmem(*shape):
         return pltpu.VMEM(shape, jnp.float32)
@@ -509,42 +556,41 @@
     return pl.pallas_call(
         functools.partial(kernel, dims),
         out_shape=pltpu.VMEM((X, Y, Z), jnp.float32),
-        in_specs=[pl.BlockSpec(memory_space=pl.ANY)] * 3,
+        in_specs=[pl.BlockSpec(memory_space=pl.ANY)] * 4,
         out_specs=pl.BlockSpec(memory_space=pltpu.VMEM),
         scratch_shapes=[
             vmem(X, Y, 128),
             vmem(X, Y, 128),
-            vmem(n, n),
+            vmem(*rw.shape),
+            vmem(*cw.shape),
             vmem(X + 10, T, 128),
             vmem(2 * (X + 8), T, 128),
             vmem(X + 8, T, 128),
-            vmem(M + 6, T1, 128),
-            vmem(U + 4, T1, 128),
+            vmem(2 * M if ring else M + 10, T1, 128),
             vmem(G, J, 128),
             vmem(2, G + 2, T, 128),
             vmem(F, J, 128),
             vmem(2, F + 2, T, 128),
-            vmem(1, J, 128),
-            vmem(2, 3, T1, 128),
-            vmem(1, J, 128),
-            vmem(2, 3, T1, 128),
+            vmem(GL, J, 128),
+            vmem(2, (2 if ring else 5) * GL, T1, 128),
             vmem(fine, 128),
             vmem(fine, 128),
             vmem(fine, 128),
             vmem(fine, 128),
             vmem(coarse, 128),
             vmem(coarse, 128),
-            vmem(16 + (M + 6) * T1, 128),
+            vmem(coarse, 128),
+            vmem(coarse, 128),
             vmem(n, 1, 128),
-            vmem(n, 128),
+            vmem(Q, 128),
             vmem(2048, 128),
-            pltpu.SemaphoreType.DMA((5,)),
-            pltpu.SemaphoreType.DMA((5,)),
-            pltpu.SemaphoreType.DMA((3,)),
+            pltpu.SemaphoreType.DMA((4,)),
+            pltpu.SemaphoreType.DMA((4,)),
+            pltpu.SemaphoreType.DMA((4,)),
         ],
         compiler_params=pltpu.CompilerParams(collective_id=0, has_side_effects=True),
         name="vcycle",
-    )(density, potential, op)
+    )(density, potential, rw, cw)
 
 
 def solution(mesh):

time: 24.9 us -> 21.7 us (0.87)
  Pallas kernels: 24.1 us -> 20.9 us
    pallas_call x1, Pallas kernels: 24.1 us -> 20.9 us  [body(): pl.pallas_call(functools.partial(kernel, dims), out_shape=pltpu.VMEM((X,...]
where the time goes in v3:
time: 21.7 us; the launch traced here: 21.6 us
  Pallas kernels  20.9 us (96%)
  local copies, waits for them, and re-layouts  0.64 us (3%)
    pallas_call x1, Pallas kernels, body(): pl.pallas_call(functools.partial(kernel, dims), out_shape=pltpu.VMEM((X,...  20.9 us
    unnamed x1, local copies, waits for them, and re-layouts  0.64 us

profile of v3, /device:TPU:0, one launch (start us, length us, event | category | flops | bytes accessed | tf_op | source)
XLA Modules:
  0.0 21.6 jit_solution(12525177567355814729)
XLA Ops:
  0.0 20.9 %vcycle.1 = f32[12,16,128]{2,1,0:T(8,128)S(1)} custom-call(f32[12,16,128]{2,1,0:T(8,128)} %den_hbm.1, f32[12,16,128]{2,1,0:T(8,128)} %pot_hbm.1, f32[18,3,8,128]{3,2,1,0:T(8,128)} %constant.4.clone.rw_hbm, f32[18,32,128]{2,1,0:T(8,128)} %constant.5.clone.cw_hbm), custom_call_target="tpu_custom_call" | custom-call | tf_op jit(solution)/shard_map/vcycle/pallas_call | solution.py:556
  20.9 0.6 %copy.6 = f32[12,16,128]{2,1,0:T(8,128)} copy(f32[12,16,128]{2,1,0:T(8,128)S(1)} %vcycle.1) | data formatting | bytes 196608

commit v4 on v3

--- a/solution.py
+++ b/solution.py
@@ -11,7 +11,8 @@
 MESH = pl.DeviceIdType.MESH
 H, H1 = 4, 12
 DEEP = 9
-SIDES = ((1, 1), (1, -1), (-1, 1), (-1, -1), (0, 1), (0, -1), (0, 0), (1, 0), (-1, 0))
+A, B_, AA, BB = 1, -1, 2, -2
+SIDES = ((1, A), (-1, A), (0, A), (1, B_), (-1, B_), (0, B_), (0, 0), (1, 0), (-1, 0))
 
 
 def table(count):
@@ -151,6 +152,22 @@
             greet(o, 0)
     else:
         each_other(greet)
+    up = {1: iy > 0, -1: iy == 0}
+
+    def along_y(d):
+        if d == 0:
+            return iy
+        return jnp.where(up[1 if d > 0 else -1], ys[abs(d)], ys[-abs(d)])
+
+    target_y = {d: along_y(d) for d in (0, 1, -1) + ((2, -2) if ny > 2 else ())}
+
+    def part_y(d, own, count, first, low=None, high=None):
+        if d == 0:
+            return first, own, first
+        low = first - count if low is None else low
+        high = first + own if high is None else high
+        goes_up = up[1 if d > 0 else -1]
+        return jnp.where(goes_up, first + own - count, first), count, jnp.where(goes_up, low, high)
 
     class Exchange:
         def __init__(self, k):
@@ -160,7 +177,7 @@
             dx, dy, dz = to
             copy = pltpu.make_async_remote_copy(
                 src_ref=src, dst_ref=dst, send_sem=ssem.at[self.k], recv_sem=rsem.at[self.k],
-                device_id=(xs[dx], ys[dy], zs[dz]), device_id_type=MESH,
+                device_id=(xs[dx], target_y[dy], zs[dz]), device_id_type=MESH,
             )
             copy.start()
             self.rows += at
@@ -259,14 +276,36 @@
 
     pl.semaphore_wait(barrier, len(steps) if near else n - 1)
     first = Exchange(0)
-    for dx, dy in SIDES:
-        if dx or dy:
-            edge = dx != 0 and dy != 0
-            block(first, cp, cp, part(dx, X, 4 if edge else 5, 5), part(dy, J, 2 if edge else 3, H), (dx, dy, 0))
-            block(first, cd, cd, part(dx, 2 * X, 5 if edge else 7, 8), part(dy, J, 2, H), (dx, dy, 0))
+
+    def trim(ex, dx, src, dst, own, at, steps, py, to):
+        seen = 0
+        for count, rows in steps:
+            px = (at + own - seen - count, count, at - seen - count) if dx == 1 else (at + seen, count, at + own + seen)
+            block(ex, src, dst, px, py(rows), to)
+            seen += count
+
+    def send_y(dy):
+        for dx in (1, -1, 0):
+            to = (dx, dy, 0)
+            if dx:
+                trim(first, dx, cp, cp, X, 5, ((2, 2), (2, 1)), lambda rows: part_y(dy, J, rows, H), to)
+                trim(first, dx, cd, cd, 2 * X, 8, ((2, 2), (3, 1)), lambda rows: part_y(dy, J, rows, H), to)
+            else:
+                block(first, cp, cp, (5, X, 5), part_y(dy, J, 3, H), to)
+                block(first, cd, cd, (8, 2 * X, 8), part_y(dy, J, 2, H), to)
+            for dz in (1, -1):
+                g0, gn, g1 = part(dx, G, 1, 1)
+                block(first, z1s, z1r, (g0 - 1, gn, g1), part_y(dy, J, 2, H), (dx, dy, dz), H, max(dz, 0))
+
+    send_y(A)
+    send_y(B_)
+    for dx in (0, 1, -1):
         for dz in (1, -1):
             g0, gn, g1 = part(dx, G, 1, 1)
-            block(first, z1s, z1r, (g0 - 1, gn, g1), part(dy, J, 2, H), (dx, dy, dz), H, max(dz, 0))
+            block(first, z1s, z1r, (g0 - 1, gn, g1), (H, J, H), (dx, 0, dz), H, max(dz, 0))
+        if dx:
+            block(first, cp, cp, part(dx, X, 5, 5), (H, J, H), (dx, 0, 0))
+            block(first, cd, cd, part(dx, 2 * X, 7, 8), (H, J, H), (dx, 0, 0))
     first.wait()
 
     def base(x, b):
@@ -377,14 +416,19 @@
         count -= own
         return (first + own - count, count, first - own - count) if d > 0 else (first, count, first + 2 * own)
 
-    ways = (2, -2, 1, -1, 0)
-    for dy in ways:
-        for dx in (1, 0) if ring else ways:
+    def deep_y(d, own, count, first):
+        if abs(d) < 2:
+            return part_y(d, own, min(own, count), first)
+        count -= own
+        return part_y(d, own, count, first, first - own - count, first + 2 * own)
+
+    for dy in (AA, BB, A, B_, 0):
+        for dx in (1, 0) if ring else (1, -1, 0, 2, -2):
             if abs(dx) + abs(dy) > 3 or (abs(dy) == 2 and J >= DEEP) or (abs(dx) == 2 and M >= E):
                 continue
             px = (0, M, M if dx else 0) if ring else deep(dx, M, E, E)
             pz = (0, GL, GL * dx) if ring else (0, GL, GL * (2 - dx))
-            py = deep(dy, J, DEEP, H1)
+            py = deep_y(dy, J, DEEP, H1)
             for dz in (1, -1):
                 block(second, zls, zlr, pz, py, (dx, dy, dz), H1, max(dz, 0))
             if dx or dy:
@@ -402,13 +446,18 @@
             ])
         zfs[f] = acc
     fourth = Exchange(3)
+    twice = nx == 2 and F == 1
     for dx, dy in SIDES:
-        if dx or dy:
-            edge = dx != 0 and dy != 0
-            block(fourth, cf, cf, part(dx, X, 3 if edge else 4, 4), part(dy, J, 2, H), (dx, dy, 0))
+        to = (dx, dy, 0)
+        if dx and dy:
+            trim(fourth, dx, cf, cf, X, 4, ((1, 2), (2, 1)), lambda rows: part_y(dy, J, rows, H), to)
+        elif dx or dy:
+            block(fourth, cf, cf, part(dx, X, 4, 4), part_y(dy, J, 2, H), to)
+        if dx == -1 and twice:
+            continue
         for dz in (1, -1):
             g0, gn, g1 = part(dx, F, 1, 1)
-            block(fourth, zfs, zfr, (g0 - 1, gn, g1), part(dy, J, 2, H), (dx, dy, dz), H, max(dz, 0))
+            block(fourth, zfs, zfr, (g0 - 1, gn, g1), part_y(dy, J, 2, H), (dx, dy, dz), H, max(dz, 0))
 
     load_cw.wait()
     others = gat.at[pl.ds(0, n - 1)]
@@ -506,7 +555,7 @@
                 far = max(-x, x - X + 1, 0)
                 z = None
                 if far < 4:
-                    f = 0 if x < 0 else (F + 1 if x >= X else x // FW + 1)
+                    f = 0 if x < 0 or (x >= X and twice) else (F + 1 if x >= X else x // FW + 1)
                     if f not in sides:
                         sides[f] = jnp.where(lane[T] < 60, zfr[0, f], zfr[1, f])
                     z = sides[f]

time: 21.7 us -> 19.9 us (0.917)
  Pallas kernels: 20.9 us -> 19.1 us
    pallas_call x1, Pallas kernels: 20.9 us -> 19.1 us  [body(): pl.pallas_call(functools.partial(kernel, dims), out_shape=pltpu.VMEM((X,...]
where the time goes in v4:
time: 19.9 us; the launch traced here: 19.8 us
  Pallas kernels  19.1 us (96%)
  local copies, waits for them, and re-layouts  0.64 us (3%)
    pallas_call x1, Pallas kernels, body(): pl.pallas_call(functools.partial(kernel, dims), out_shape=pltpu.VMEM((X,...  19.1 us
    unnamed x1, local copies, waits for them, and re-layouts  0.64 us

profile of v4, /device:TPU:0, one launch (start us, length us, event | category | flops | bytes accessed | tf_op | source)
XLA Modules:
  0.0 19.8 jit_solution(658588813580711918)
XLA Ops:
  0.0 19.1 %vcycle.1 = f32[12,16,128]{2,1,0:T(8,128)S(1)} custom-call(f32[12,16,128]{2,1,0:T(8,128)} %den_hbm.1, f32[12,16,128]{2,1,0:T(8,128)} %pot_hbm.1, f32[18,3,8,128]{3,2,1,0:T(8,128)} %constant.4.clone.rw_hbm, f32[18,32,128]{2,1,0:T(8,128)} %constant.5.clone.cw_hbm), custom_call_target="tpu_custom_call" | custom-call | tf_op jit(solution)/shard_map/vcycle/pallas_call | solution.py:605
  19.1 0.6 %copy.6 = f32[12,16,128]{2,1,0:T(8,128)} copy(f32[12,16,128]{2,1,0:T(8,128)S(1)} %vcycle.1) | data formatting | bytes 196608

commit v5 on v4

--- a/solution.py
+++ b/solution.py
@@ -87,8 +87,8 @@
 
 def kernel(
     dims, den_hbm, pot_hbm, rw_hbm, cw_hbm, out_ref,
-    den_v, pot_v, rw, cw, cp, cd, cf, cl,
-    z1s, z1r, zfs, zfr, zls, zlr,
+    den_v, pot_v, rw, cw, cp, cpy, cd, cdy, cf, cl,
+    z1s, z1r, z1y, zfs, zfr, zls, zlr,
     R, B, SR, SB, LR, LB, ER, EB, gat, cv, dummy,
     ssem, rsem, lsem,
 ):
@@ -131,10 +131,6 @@
     load_d = pltpu.make_async_copy(den_hbm, wide(den_v), lsem.at[1])
     load_rw = pltpu.make_async_copy(rw_hbm, rw, lsem.at[2])
     load_cw = pltpu.make_async_copy(cw_hbm, cw, lsem.at[3])
-    load_p.start()
-    load_d.start()
-    load_rw.start()
-    load_cw.start()
 
     barrier = pltpu.get_barrier_semaphore()
 
@@ -148,10 +144,15 @@
         for dx in (-1, 0, 1) for dy in (-1, 0, 1) for dz in (-1, 0, 1)
     } - {0})
     if near:
-        for o in steps:
+        for o in sorted(steps, key=lambda o: o // nz % ny == 0):
             greet(o, 0)
     else:
         each_other(greet)
+    load_p.start()
+    load_d.start()
+    load_rw.start()
+    load_cw.start()
+
     up = {1: iy > 0, -1: iy == 0}
 
     def along_y(d):
@@ -206,7 +207,7 @@
     def iota(rows, dim):
         return lax.broadcasted_iota(jnp.int32, (rows, 128), dim)
 
-    lane = {rows: iota(rows, 1) for rows in {J, T, T1}}
+    lane = {rows: iota(rows, 1) for rows in {8, J, T, T1}}
 
     def place(acc, v, pieces):
         by_shift = {}
@@ -246,9 +247,26 @@
         take = [jnp.take_along_axis(u, order[which], axis=1, mode="promise_in_bounds") for u in v]
         return jnp.where(l8 < K, take[0], take[1])
 
+    def plane(x, deep):
+        if 0 <= x < X:
+            return (x + X // 2) % X
+        return X + deep + x if x < 0 else deep + x
+
     def tile(x, t):
-        forward = 0 <= x < X // 2 or x >= X
-        return 2 * (x + 4) + (t if forward else 1 - t)
+        if 0 <= x < X:
+            return 2 * plane(x, 4) + (t if x < X // 2 else 1 - t)
+        return 2 * X + (6 + 2 * (x + 1) - t if x < 0 else 7 + 2 * (x - X) + t)
+
+    def group(g):
+        return 0 if g < 0 else (1 if g >= G else 2 + (g + 1) % G)
+
+    def along_x(count, middle, halo, halo_size):
+        if nx == 2:
+            return [(1, (middle - count, 2 * count, halo + halo_size - count))]
+        return [(1, (middle - count, count, halo + halo_size - count)), (-1, (middle, count, halo + halo_size))]
+
+    def groups_x():
+        return [(1, (0, 2, 0))] if nx == 2 else [(1, (0, 1, 0)), (-1, (1, 1, 1))]
 
     load_p.wait()
     load_d.wait()
@@ -259,54 +277,51 @@
             x = 4 * g + q
             black = colours(pot_v, x, 1 - x % 2)
             dens = [colours(den_v, x, x % 2), colours(den_v, x, 1 - x % 2)]
-            cp[x + 5, H : H + J] = black
+            cp[plane(x, 5)] = black
             acc = place(acc, black, [
                 p for h in (0, 1)
                 for p in ((h * K, 15 * q + 3 * h, 3), (h * K + K - 3, 61 + 15 * q + 3 * h, 3))
             ])
             for t in (0, 1):
-                cd[tile(x, t), H : H + J] = dens[t]
+                cd[tile(x, t)] = dens[t]
                 total = total + dens[t]
                 acc = place(acc, dens[t], [
                     p for h in (0, 1) for o in (15 * q + 6 + 4 * t + 2 * h,)
                     for p in ((h * K, o, 2), (h * K + K - 2, 62 + o, 2))
                 ])
-        z1s[g] = acc
+        z1s[(g + 1) % G] = acc
     total = jnp.where(l8 < 2 * K, total, 0.0)
 
     pl.semaphore_wait(barrier, len(steps) if near else n - 1)
-    first = Exchange(0)
-
-    def trim(ex, dx, src, dst, own, at, steps, py, to):
-        seen = 0
-        for count, rows in steps:
-            px = (at + own - seen - count, count, at - seen - count) if dx == 1 else (at + seen, count, at + own + seen)
-            block(ex, src, dst, px, py(rows), to)
-            seen += count
-
-    def send_y(dy):
-        for dx in (1, -1, 0):
-            to = (dx, dy, 0)
-            if dx:
-                trim(first, dx, cp, cp, X, 5, ((2, 2), (2, 1)), lambda rows: part_y(dy, J, rows, H), to)
-                trim(first, dx, cd, cd, 2 * X, 8, ((2, 2), (3, 1)), lambda rows: part_y(dy, J, rows, H), to)
-            else:
-                block(first, cp, cp, (5, X, 5), part_y(dy, J, 3, H), to)
-                block(first, cd, cd, (8, 2 * X, 8), part_y(dy, J, 2, H), to)
+    first, first_y = Exchange(0), Exchange(3)
+
+    def rim(dy, rows, skip=0):
+        return part_y(dy, J - skip, rows, 0, 8 - skip - rows, skip) if not skip else (
+            jnp.where(up[dy], J - skip - rows, skip), rows, jnp.where(up[dy], 8 - skip - rows, skip))
+
+    for dy in (A, B_):
+        for count, skip in ((4, 0), (2, 1)):
+            for dx, px in along_x(count, X // 2, X, 5):
+                block(first_y, cp, cpy, px, rim(dy, 1, skip), (dx, dy, 0))
+        for count, skip in ((5, 0), (2, 1)):
+            for dx, px in along_x(count, X, 2 * X, 7):
+                block(first_y, cd, cdy, px, rim(dy, 1, skip), (dx, dy, 0))
+        for dx, px in groups_x():
             for dz in (1, -1):
-                g0, gn, g1 = part(dx, G, 1, 1)
-                block(first, z1s, z1r, (g0 - 1, gn, g1), part_y(dy, J, 2, H), (dx, dy, dz), H, max(dz, 0))
-
-    send_y(A)
-    send_y(B_)
-    for dx in (0, 1, -1):
+                block(first_y, z1s, z1y, px, rim(dy, 2), (dx, dy, dz), 0, max(dz, 0))
+        block(first_y, cp, cpy, (0, X, 0), rim(dy, 3), (0, dy, 0))
+        block(first_y, cd, cdy, (0, 2 * X, 0), rim(dy, 2), (0, dy, 0))
         for dz in (1, -1):
-            g0, gn, g1 = part(dx, G, 1, 1)
-            block(first, z1s, z1r, (g0 - 1, gn, g1), (H, J, H), (dx, 0, dz), H, max(dz, 0))
-        if dx:
-            block(first, cp, cp, part(dx, X, 5, 5), (H, J, H), (dx, 0, 0))
-            block(first, cd, cd, part(dx, 2 * X, 7, 8), (H, J, H), (dx, 0, 0))
-    first.wait()
+            block(first_y, z1s, z1y, (0, G, 2), rim(dy, 2), (0, dy, dz), 0, max(dz, 0))
+    whole_rows = (0, J, 0)
+    for dz in (1, -1):
+        block(first, z1s, z1r, (0, G, 2), whole_rows, (0, 0, dz), 0, max(dz, 0))
+        for dx, px in groups_x():
+            block(first, z1s, z1r, px, whole_rows, (dx, 0, dz), 0, max(dz, 0))
+    for dx, px in along_x(5, X // 2, X, 5):
+        block(first, cp, cp, px, whole_rows, (dx, 0, 0))
+    for dx, px in along_x(7, X, 2 * X, 7):
+        block(first, cd, cd, px, whole_rows, (dx, 0, 0))
 
     def base(x, b):
         return 8 + ((x + 5) * 2 + b) * T
@@ -319,23 +334,42 @@
 
     sides = {}
 
-    def side(x):
-        g = x // 4 + 1
-        if g not in sides:
-            sides[g] = jnp.where(lane[T] < 60, z1r[0, g], z1r[1, g])
-        return sides[g]
-
-    for x in range(-5, X + 5):
-        far = max(-x, x - X + 1, 0)
-        z = side(x) if far < 5 else None
-        for h in (0, 1):
-            s = 15 * (x % 4) + 3 * h
-            B[pl.ds(base(x, h), T), :] = with_sides(cp[x + 5], h, z, K - s, 64 - s)
-        for t, ref in ((0, SR), (1, SB)):
-            if far <= 4 - t:
+    def side(x, ref, rows):
+        key = (x // 4, rows)
+        if key not in sides:
+            sides[key] = jnp.where(lane[rows] < 60, ref[0, group(key[0])], ref[1, group(key[0])])
+        return sides[key]
+
+    def unpack(tiles, dens, zs_, rows, less, put):
+        for x in range(-5, X + 5):
+            far = max(-x, x - X + 1, 0) + less
+            z = side(x, zs_, rows) if far < 5 else None
+            if far <= 5:
                 for h in (0, 1):
-                    s = 15 * (x % 4) + 6 + 4 * t + 2 * h
-                    ref[pl.ds(base(x, h), T), :] = with_sides(cd[tile(x, t)], h, z, K - s, 64 - s)
+                    s = 15 * (x % 4) + 3 * h
+                    put(B, x, h, with_sides(tiles[plane(x, 5)], h, z, K - s, 64 - s))
+            for t, ref in ((0, SR), (1, SB)):
+                z = side(x, zs_, rows) if far < 4 - t else None
+                if far <= 4 - t:
+                    for h in (0, 1):
+                        s = 15 * (x % 4) + 6 + 4 * t + 2 * h
+                        put(ref, x, h, with_sides(dens[tile(x, t)], h, z, K - s, 64 - s))
+
+    def put_middle(ref, x, h, v):
+        ref[pl.ds(base(x, h) + H, J), :] = v
+
+    def put_rim(ref, x, h, v):
+        ref[pl.ds(base(x, h) + H - 3, 3), :] = v[5:8]
+        ref[pl.ds(base(x, h) + H + J, 3), :] = v[0:3]
+
+    load_rw.wait()
+    load_cw.wait()
+    first.wait()
+    unpack(cp, cd, z1r, J, 0, put_middle)
+    first_y.wait()
+    sides.clear()
+    unpack(cpy, cdy, z1y, 8, 1, put_rim)
+    sides.clear()
 
     sixth = jnp.float32(1.0 / 6.0)
 
@@ -368,7 +402,6 @@
                     r = own(s, x, b) - (beside(own, w, x, b, colour) - 6.0 * own(v, x, b))
                     left = r if left is None else left + r
         one.append(left * 0.5)
-    load_rw.wait()
     sums = [jnp.zeros((J, 128), jnp.float32) for _ in names]
     for g in range(GL):
         acc = jnp.zeros((J, 128), jnp.float32)
@@ -406,7 +439,24 @@
         ).start()
         return carry
 
-    each_other(spread)
+    def spread_y(d):
+        for dx in range(nx):
+            for dz in range(nz):
+                if d == 0 and dx == 0 and dz == 0:
+                    continue
+                slot = [(-dx % nx * ny + dy % ny) * nz + -dz % nz for dy in (-abs(d), abs(d))]
+                there = jnp.where(up[d], slot[0], slot[1]) if abs(d) == 1 else slot[0]
+                where_y = target_y[d] if abs(d) == 1 else ys[d]
+                pltpu.make_async_remote_copy(
+                    src_ref=gat.at[0], dst_ref=gat.at[there], send_sem=ssem.at[2], recv_sem=rsem.at[2],
+                    device_id=(xs[dx], where_y, zs[dz]), device_id_type=MESH,
+                ).start()
+
+    by_rows = n <= 64 and ny > 2
+    if by_rows:
+        spread_y(A)
+    else:
+        each_other(spread)
 
     second = Exchange(1)
 
@@ -422,7 +472,7 @@
         count -= own
         return part_y(d, own, count, first, first - own - count, first + 2 * own)
 
-    for dy in (AA, BB, A, B_, 0):
+    def send_deep(dy):
         for dx in (1, 0) if ring else (1, -1, 0, 2, -2):
             if abs(dx) + abs(dy) > 3 or (abs(dy) == 2 and J >= DEEP) or (abs(dx) == 2 and M >= E):
                 continue
@@ -434,32 +484,41 @@
             if dx or dy:
                 block(second, cl, cl, px, py, (dx, dy, 0))
 
+    send_deep(A)
+    if by_rows:
+        for d in range(2, ny - 1):
+            spread_y(d)
+        spread_y(B_)
+    send_deep(AA)
+    send_deep(BB)
+    send_deep(B_)
+    send_deep(0)
+    if by_rows:
+        spread_y(0)
+
     for f in range(F):
         acc = jnp.zeros((J, 128), jnp.float32)
         for q in range(FW):
             x = f * FW + q
             v = two(own(B, x, 0), own(B, x, 1))
-            cf[x + 4, H : H + J] = v
+            cf[plane(x, 4), H : H + J] = v
             acc = place(acc, v, [
                 p for h in (0, 1) for o in (4 * q + 2 * h,)
                 for p in ((h * K, o, 2), (h * K + K - 2, 62 + o, 2))
             ])
         zfs[f] = acc
-    fourth = Exchange(3)
+    fourth = Exchange(4)
     twice = nx == 2 and F == 1
-    for dx, dy in SIDES:
-        to = (dx, dy, 0)
-        if dx and dy:
-            trim(fourth, dx, cf, cf, X, 4, ((1, 2), (2, 1)), lambda rows: part_y(dy, J, rows, H), to)
-        elif dx or dy:
-            block(fourth, cf, cf, part(dx, X, 4, 4), part_y(dy, J, 2, H), to)
-        if dx == -1 and twice:
-            continue
-        for dz in (1, -1):
-            g0, gn, g1 = part(dx, F, 1, 1)
-            block(fourth, zfs, zfr, (g0 - 1, gn, g1), part_y(dy, J, 2, H), (dx, dy, dz), H, max(dz, 0))
-
-    load_cw.wait()
+    for dy in (A, B_, 0):
+        for dx, px in along_x(3 if dy else 4, X // 2, X, 4):
+            block(fourth, cf, cf, px, part_y(dy, J, 2, H), (dx, dy, 0))
+        if dy:
+            block(fourth, cf, cf, (0, X, 0), part_y(dy, J, 2, H), (0, dy, 0))
+        for dx in (1, 0) if twice else (1, -1, 0):
+            for dz in (1, -1):
+                g0, gn, g1 = part(dx, F, 1, 1)
+                block(fourth, zfs, zfr, (g0 - 1, gn, g1), part_y(dy, J, 2, H), (dx, dy, dz), H, max(dz, 0))
+
     others = gat.at[pl.ds(0, n - 1)]
     pltpu.make_async_copy(others, others, rsem.at[2]).wait()
     pltpu.make_async_copy(others, others, ssem.at[2]).wait()
@@ -506,9 +565,6 @@
             s = 18 * q + 9 * c
             ref[pl.ds(base1(m), T1), :] = with_sides(cl[m + E], c, sides[g], K - s, 64 - s)
 
-    for m in span(DEEP):
-        ER[pl.ds(base1(m), T1), :] = get1(LR, m, 0, T1) * -sixth
-
     masks = {}
 
     def even_from(start, rows):
@@ -516,8 +572,10 @@
             masks[rows] = (lax.broadcasted_iota(jnp.int32, (rows, 128), 0) + lax.broadcasted_iota(jnp.int32, (rows, 128), 1)) % 2 == 0
         return masks[rows] if start % 2 == 0 else jnp.logical_not(masks[rows])
 
-    def half1(depth, colour, shift=None, first=False):
+    def half1(depth, colour, shift=None, start_red=False):
         new, old, src = ((ER, EB, LR), (EB, ER, LB))[colour]
+        if start_red:
+            old = LR
         start, rows = window(depth)
         mask = even_from(start, rows)
         for m in span(depth):
@@ -525,12 +583,13 @@
             before, after = get1(old, m - 1, start, rows), get1(old, m + 1, start, rows)
             t = c + (jnp.where(mask, before, after) if colour == 0 else jnp.where(mask, after, before))
             t = t + (get1(old, m, start - 1, rows) + get1(old, m, start + 1, rows))
-            t = t + (turn(c, 1) + turn(c, -1)) - get1(src, m, start, rows)
+            t = t + (turn(c, 1) + turn(c, -1))
+            t = (t * -sixth if start_red else t) - get1(src, m, start, rows)
             if shift is not None:
                 t = t + shift
             new[pl.ds(base1(m) + start, rows), :] = t * sixth
 
-    half1(8, 1)
+    half1(8, 1, start_red=True)
     half1(7, 0)
     half1(6, 1)
     for m in span(6):
@@ -561,7 +620,7 @@
                     z = sides[f]
                 for h in (0, 1):
                     s = 4 * (x % FW) + 2 * h
-                    B[pl.ds(base(x, h), T), :] = with_sides(cf[x + 4], h, z, K - s, 64 - s) + e
+                    B[pl.ds(base(x, h), T), :] = with_sides(cf[plane(x, 4)], h, z, K - s, 64 - s) + e
 
     def last(depth, colour):
         new, old, src = ((R, B, SR), (B, R, SB))[colour]
@@ -612,12 +671,15 @@
             vmem(X, Y, 128),
             vmem(*rw.shape),
             vmem(*cw.shape),
-            vmem(X + 10, T, 128),
-            vmem(2 * (X + 8), T, 128),
+            vmem(X + 10, J, 128),
+            vmem(X + 10, 8, 128),
+            vmem(2 * X + 14, J, 128),
+            vmem(2 * X + 14, 8, 128),
             vmem(X + 8, T, 128),
             vmem(2 * M if ring else M + 10, T1, 128),
             vmem(G, J, 128),
-            vmem(2, G + 2, T, 128),
+            vmem(2, G + 2, J, 128),
+            vmem(2, G + 2, 8, 128),
             vmem(F, J, 128),
             vmem(2, F + 2, T, 128),
             vmem(GL, J, 128),
@@ -633,8 +695,8 @@
             vmem(n, 1, 128),
             vmem(Q, 128),
             vmem(2048, 128),
-            pltpu.SemaphoreType.DMA((4,)),
-            pltpu.SemaphoreType.DMA((4,)),
+            pltpu.SemaphoreType.DMA((5,)),
+            pltpu.SemaphoreType.DMA((5,)),
             pltpu.SemaphoreType.DMA((4,)),
         ],
         compiler_params=pltpu.CompilerParams(collective_id=0, has_side_effects=True),

time: 19.9 us -> 19.6 us (0.985)
  Pallas kernels: 19.1 us -> 18.9 us
    pallas_call x1, Pallas kernels: 19.1 us -> 18.9 us  [body(): pl.pallas_call(functools.partial(kernel, dims), out_shape=pltpu.VMEM((X,...]
where the time goes in v5:
time: 19.6 us; the launch traced here: 19.5 us
  Pallas kernels  18.9 us (96%)
  local copies, waits for them, and re-layouts  0.64 us (3%)
    pallas_call x1, Pallas kernels, body(): pl.pallas_call(functools.partial(kernel, dims), out_shape=pltpu.VMEM((X,...  18.9 us
    unnamed x1, local copies, waits for them, and re-layouts  0.64 us

profile of v5, /device:TPU:0, one launch (start us, length us, event | category | flops | bytes accessed | tf_op | source)
XLA Modules:
  0.0 19.5 jit_solution(11866496942235562154)
XLA Ops:
  0.0 18.9 %vcycle.1 = f32[12,16,128]{2,1,0:T(8,128)S(1)} custom-call(f32[12,16,128]{2,1,0:T(8,128)} %den_hbm.1, f32[12,16,128]{2,1,0:T(8,128)} %pot_hbm.1, f32[18,3,8,128]{3,2,1,0:T(8,128)} %constant.4.clone.rw_hbm, f32[18,32,128]{2,1,0:T(8,128)} %constant.5.clone.cw_hbm), custom_call_target="tpu_custom_call" | custom-call | tf_op jit(solution)/shard_map/vcycle/pallas_call | solution.py:664
  18.9 0.6 %copy.6 = f32[12,16,128]{2,1,0:T(8,128)} copy(f32[12,16,128]{2,1,0:T(8,128)S(1)} %vcycle.1) | data formatting | bytes 196608

commit v6 on v5

--- a/solution.py
+++ b/solution.py
@@ -153,7 +153,7 @@
     load_rw.start()
     load_cw.start()
 
-    up = {1: iy > 0, -1: iy == 0}
+    up = {1: 2 * iy >= ny, -1: 2 * iy < ny}
 
     def along_y(d):
         if d == 0:
@@ -300,19 +300,19 @@
             jnp.where(up[dy], J - skip - rows, skip), rows, jnp.where(up[dy], 8 - skip - rows, skip))
 
     for dy in (A, B_):
+        for dx, px in groups_x():
+            for dz in (1, -1):
+                block(first_y, z1s, z1y, px, rim(dy, 2), (dx, dy, dz), 0, max(dz, 0))
         for count, skip in ((4, 0), (2, 1)):
             for dx, px in along_x(count, X // 2, X, 5):
                 block(first_y, cp, cpy, px, rim(dy, 1, skip), (dx, dy, 0))
         for count, skip in ((5, 0), (2, 1)):
             for dx, px in along_x(count, X, 2 * X, 7):
                 block(first_y, cd, cdy, px, rim(dy, 1, skip), (dx, dy, 0))
-        for dx, px in groups_x():
-            for dz in (1, -1):
-                block(first_y, z1s, z1y, px, rim(dy, 2), (dx, dy, dz), 0, max(dz, 0))
+        for dz in (1, -1):
+            block(first_y, z1s, z1y, (0, G, 2), rim(dy, 2), (0, dy, dz), 0, max(dz, 0))
         block(first_y, cp, cpy, (0, X, 0), rim(dy, 3), (0, dy, 0))
         block(first_y, cd, cdy, (0, 2 * X, 0), rim(dy, 2), (0, dy, 0))
-        for dz in (1, -1):
-            block(first_y, z1s, z1y, (0, G, 2), rim(dy, 2), (0, dy, dz), 0, max(dz, 0))
     whole_rows = (0, J, 0)
     for dz in (1, -1):
         block(first, z1s, z1r, (0, G, 2), whole_rows, (0, 0, dz), 0, max(dz, 0))
@@ -583,10 +583,9 @@
             before, after = get1(old, m - 1, start, rows), get1(old, m + 1, start, rows)
             t = c + (jnp.where(mask, before, after) if colour == 0 else jnp.where(mask, after, before))
             t = t + (get1(old, m, start - 1, rows) + get1(old, m, start + 1, rows))
-            t = t + (turn(c, 1) + turn(c, -1))
-            t = (t * -sixth if start_red else t) - get1(src, m, start, rows)
-            if shift is not None:
-                t = t + shift
+            beside_z = turn(c, 1) + turn(c, -1)
+            rest = get1(src, m, start, rows) if shift is None else get1(src, m, start, rows) - shift
+            t = (t + beside_z) * -sixth - rest if start_red else (t - rest) + beside_z
             new[pl.ds(base1(m) + start, rows), :] = t * sixth
 
     half1(8, 1, start_red=True)

time: 19.6 us -> 19.6 us (level)
  no operation moved by 1% of the time
where the time goes in v6:
time: 19.6 us; the launch traced here: 19.5 us
  Pallas kernels  18.8 us (96%)
  local copies, waits for them, and re-layouts  0.64 us (3%)
    pallas_call x1, Pallas kernels, body(): pl.pallas_call(functools.partial(kernel, dims), out_shape=pltpu.VMEM((X,...  18.8 us
    unnamed x1, local copies, waits for them, and re-layouts  0.64 us

profile of v6, /device:TPU:0, one launch (start us, length us, event | category | flops | bytes accessed | tf_op | source)
XLA Modules:
  0.0 19.5 jit_solution(16227231487953661944)
XLA Ops:
  0.0 18.8 %vcycle.1 = f32[12,16,128]{2,1,0:T(8,128)S(1)} custom-call(f32[12,16,128]{2,1,0:T(8,128)} %den_hbm.1, f32[12,16,128]{2,1,0:T(8,128)} %pot_hbm.1, f32[18,3,8,128]{3,2,1,0:T(8,128)} %constant.4.clone.rw_hbm, f32[18,32,128]{2,1,0:T(8,128)} %constant.5.clone.cw_hbm), custom_call_target="tpu_custom_call" | custom-call | tf_op jit(solution)/shard_map/vcycle/pallas_call | solution.py:663
  18.8 0.6 %copy.6 = f32[12,16,128]{2,1,0:T(8,128)} copy(f32[12,16,128]{2,1,0:T(8,128)S(1)} %vcycle.1) | data formatting | bytes 196608

commit v7 on v6

--- a/solution.py
+++ b/solution.py
@@ -510,8 +510,12 @@
     fourth = Exchange(4)
     twice = nx == 2 and F == 1
     for dy in (A, B_, 0):
-        for dx, px in along_x(3 if dy else 4, X // 2, X, 4):
-            block(fourth, cf, cf, px, part_y(dy, J, 2, H), (dx, dy, 0))
+        for count, row in ((3, 0), (1, 1)) if dy else ((4, 0),):
+            for dx, px in along_x(count, X // 2, X, 4):
+                py = part_y(dy, J, J, H)
+                if dy:
+                    py = (jnp.where(up[dy], H + J - 1 - row, H + row), 1, jnp.where(up[dy], H - 1 - row, H + J + row))
+                block(fourth, cf, cf, px, py, (dx, dy, 0))
         if dy:
             block(fourth, cf, cf, (0, X, 0), part_y(dy, J, 2, H), (0, dy, 0))
         for dx in (1, 0) if twice else (1, -1, 0):

time: 19.6 us -> 19.6 us (level)
  no operation moved by 1% of the time
where the time goes in v7:
time: 19.6 us; the launch traced here: 19.4 us
  Pallas kernels  18.8 us (96%)
  local copies, waits for them, and re-layouts  0.64 us (3%)
    pallas_call x1, Pallas kernels, body(): pl.pallas_call(functools.partial(kernel, dims), out_shape=pltpu.VMEM((X,...  18.8 us
    unnamed x1, local copies, waits for them, and re-layouts  0.64 us

profile of v7, /device:TPU:0, one launch (start us, length us, event | category | flops | bytes accessed | tf_op | source)
XLA Modules:
  0.0 19.4 jit_solution(623561321507789197)
XLA Ops:
  0.0 18.8 %vcycle.1 = f32[12,16,128]{2,1,0:T(8,128)S(1)} custom-call(f32[12,16,128]{2,1,0:T(8,128)} %den_hbm.1, f32[12,16,128]{2,1,0:T(8,128)} %pot_hbm.1, f32[18,3,8,128]{3,2,1,0:T(8,128)} %constant.4.clone.rw_hbm, f32[18,32,128]{2,1,0:T(8,128)} %constant.5.clone.cw_hbm), custom_call_target="tpu_custom_call" | custom-call | tf_op jit(solution)/shard_map/vcycle/pallas_call | solution.py:667
  18.8 0.6 %copy.6 = f32[12,16,128]{2,1,0:T(8,128)} copy(f32[12,16,128]{2,1,0:T(8,128)S(1)} %vcycle.1) | data formatting | bytes 196608
